TPU v7x, 32 devices: a whole 2x2x4 slice. The times are simulated.
32 devices in a mesh: px: 2 (over core), py: 4 (over z), ta: 4 (over y, x).
Axes of the slice: x: 2, y: 2, z: 4, core: 2. Of those that a mesh axis runs over, the one named last changes fastest.
Arguments:
- snapshots: bfloat16 [384, 5, 65536], P('ta', None, ('px', 'py')), may hold values from -6 to 6
- quad_weights: float32 [65536], P(('px', 'py')), may hold values from 1 to 10
- spectral_indices: int32 [32], replicated, may hold values from 0 to 127
Outputs:
- spectra: float32 [32, 2, 2, 5, 65536], P('ta', None, None, None, ('px', 'py'))
- gram: float32 [32, 2, 2, 2], P('ta')
All inputs are finite; a program needn't handle non-finite values.
Results may differ from a plain program's by a relative error of at most 0.0042.
Values may be sent and summed in bfloat16 or wider, within the bound.
A program may use at most 128 MiB of HBM per device.

v0:
```python
import functools
import math

import jax
import jax.numpy as jnp
from jax import lax
from jax.experimental import pallas as pl
from jax.experimental.pallas import tpu as pltpu
from jax.sharding import PartitionSpec as P

VARS = 5
BLK = 256
HOP = 128
SEGMENT_NUMBER = 2
RETAINED_MODES = 32

MESH = pl.DeviceIdType.MESH


def make_rotation_multipliers(spectral_indices, temporal_locations):
    segment_beginnings = jnp.arange(SEGMENT_NUMBER, dtype=jnp.int32) * HOP
    segment_shifts = temporal_locations[None, :] - segment_beginnings[:, None]
    inside = (segment_shifts >= 0) & (segment_shifts < BLK)
    window = 0.5 - 0.5 * jnp.cos(2.0 * math.pi * segment_shifts.astype(jnp.float32) / BLK)
    window = jnp.where(inside, window, jnp.float32(0.0)) / jnp.sqrt(jnp.float32(3.0 * BLK / 8.0))
    phases = jnp.mod(spectral_indices[:, None, None] * segment_shifts[None, :, :], BLK)
    angles = 2.0 * math.pi * phases.astype(jnp.float32) / BLK
    real_part = jnp.cos(angles) * window[None]
    imag_part = -jnp.sin(angles) * window[None]
    gathered_segments = jnp.stack([real_part, imag_part], axis=2)
    return gathered_segments.reshape(
        RETAINED_MODES * SEGMENT_NUMBER * 2, temporal_locations.shape[0]
    ).astype(jnp.bfloat16)


def gram_terms(spectra):
    flat = spectra.reshape(spectra.shape[0], 2 * SEGMENT_NUMBER, -1)
    inner = jnp.einsum("fam,fbm->fab", flat, flat, precision=lax.Precision.HIGHEST)
    inner = inner.reshape(spectra.shape[0], SEGMENT_NUMBER, 2, SEGMENT_NUMBER, 2)
    real_part = inner[:, :, 0, :, 0] + inner[:, :, 1, :, 1]
    imag_part = inner[:, :, 0, :, 1] - inner[:, :, 1, :, 0]
    return jnp.stack([real_part, imag_part], axis=-1)


def plain_on_device(snapshots, quad_weights, spectral_indices):
    record_length = snapshots.shape[0]
    point_count = snapshots.shape[2]
    groups = lax.axis_size("ta")
    temporal_locations = lax.axis_index("ta") * record_length + jnp.arange(
        record_length, dtype=jnp.int32
    )
    rotation_multipliers = make_rotation_multipliers(spectral_indices, temporal_locations)
    flat_snapshots = snapshots.reshape(record_length, VARS * point_count)
    raw = lax.psum_scatter(
        jnp.dot(rotation_multipliers, flat_snapshots, preferred_element_type=jnp.float32),
        "ta",
        scatter_dimension=0,
        tiled=True,
    )
    raw = raw.reshape(RETAINED_MODES // groups, SEGMENT_NUMBER, 2, VARS, point_count)
    spectra = raw * jnp.sqrt(quad_weights)
    summed = lax.psum(gram_terms(spectra), ("px", "py"))
    total_points = point_count * lax.axis_size("px") * lax.axis_size("py")
    gram = summed / jnp.float32(total_points * VARS)
    return (spectra, gram)


def sine_of_turn(m):
    quarter = BLK // 4
    r = jnp.bitwise_and(m + quarter, BLK - 1) - quarter
    r = jnp.where(r > quarter, BLK // 2 - r, r)
    x = r.astype(jnp.float32) * (2.0 * math.pi / BLK)
    y = x * x
    total = jnp.full_like(x, -1.0 / math.factorial(11))
    for n in (9, 7, 5, 3, 1):
        total = total * y + (1.0 if n % 4 == 1 else -1.0) / math.factorial(n)
    return total * x


def window_kernel(
    pieces, tail, tile, gram_scale,
    snap_hbm, weight_hbm, index_hbm, out_ref, gram_ref,
    snap, index_ref, weight_ref, twiddle, own, root,
    a_send, a_recv, n1_send, n1_recv, n2_send, n2_recv, m1_send, m1_recv,
    acc, gram_send, gram_recv,
    load_sem, index_sem, weight_sem,
    a_ssem, a_rsem, n1_ssem, n1_rsem, n2_ssem, n2_rsem, m1_ssem, m1_rsem,
    gram_ssem, gram_rsem,
):
    px, py, ta = lax.axis_index("px"), lax.axis_index("py"), lax.axis_index("ta")
    npx, npy = lax.axis_size("px"), lax.axis_size("py")
    variables, record, points = snap_hbm.shape
    modes = out_ref.shape[0]
    unit = 2 * modes
    steps = variables * pieces
    span = points // pieces
    half = span // 2
    short = span // tail
    f32, bf16 = jnp.float32, jnp.bfloat16

    inner = (ta == 1) | (ta == 2)
    outer = jnp.logical_not(inner)
    me = jnp.where(inner, ta - 1, ta // 3)
    sides = (jnp.where(inner, 0, 1), jnp.where(inner, 3, 2))

    def load(variable):
        return pltpu.make_async_copy(snap_hbm.at[variable], snap.at[variable], load_sem.at[variable])

    index_copy = pltpu.make_async_copy(index_hbm, index_ref, index_sem)
    weight_copy = pltpu.make_async_copy(weight_hbm, weight_ref, weight_sem)
    index_copy.start()

    peers = [
        (i, j, lax.rem(px + i, npx), lax.rem(py + j, npy))
        for i in range(npx) for j in range(npy) if i + j > 0
    ]
    barrier = pltpu.get_barrier_semaphore()
    for side in sides:
        pl.semaphore_signal(barrier, inc=1, device_id=(px, py, side), device_id_type=MESH)
    for _, _, x, y in peers:
        pl.semaphore_signal(barrier, inc=1, device_id=(x, y, ta), device_id_type=MESH)

    for variable in range(variables):
        load(variable).start()
    weight_copy.start()

    sublane = lax.broadcasted_iota(jnp.int32, (modes, record), 0)
    moment = lax.broadcasted_iota(jnp.int32, (modes, record), 1) + ta * record
    shifts, windows = [], []
    for block in range(SEGMENT_NUMBER):
        shift = moment - block * HOP
        inside = (shift >= 0) & (shift < BLK)
        hann = 0.5 - 0.5 * sine_of_turn(shift + BLK // 4)
        shifts.append(shift)
        windows.append(jnp.where(inside, hann, 0.0) / math.sqrt(3.0 * BLK / 8.0))
    index_copy.wait()
    for place, owner in enumerate((3 - ta, sides[0], sides[1], ta)):
        bins = jnp.zeros((modes, record), jnp.int32)
        for f in range(modes):
            bins = jnp.where(sublane == f, index_ref[owner * modes + f], bins)
        for block in range(SEGMENT_NUMBER):
            shift, hann = shifts[block], windows[block]
            phase = bins * shift
            rows = jnp.concatenate(
                [sine_of_turn(phase + BLK // 4) * hann, -sine_of_turn(phase) * hann], axis=0)
            if place < 3:
                at = jnp.where(inner, place * SEGMENT_NUMBER + block, block * 3 + place)
                twiddle[pl.ds(pl.multiple_of(at * unit, unit), unit), :] = rows.astype(bf16)
            else:
                own[block * unit:(block + 1) * unit, :] = rows.astype(bf16)
    acc[...] = jnp.zeros_like(acc)

    def remote(send, recv, ssem, rsem, side, *at):
        return pltpu.make_async_remote_copy(
            src_ref=send.at[(side, *at)], dst_ref=recv.at[(me, *at)],
            send_sem=ssem.at[side, at[0]], recv_sem=rsem.at[me, at[0]],
            device_id=(px, py, sides[side]), device_id_type=MESH,
        )

    def landed(send, recv, ssem, rsem, side, *at):
        return pltpu.make_async_remote_copy(
            src_ref=send.at[(side, *at)], dst_ref=recv.at[(side, *at)],
            send_sem=ssem.at[side, at[0]], recv_sem=rsem.at[side, at[0]],
            device_id=(px, py, sides[side]), device_id_type=MESH,
        )

    a_refs = (a_send, a_recv, a_ssem, a_rsem)
    n1_refs = (n1_send, n1_recv, n1_ssem, n1_rsem)
    n2_refs = (n2_send, n2_recv, n2_ssem, n2_rsem)

    def m1_copy(here, side, k, n=None):
        send, recv, ssem, rsem = m1_send.at[side, k], m1_recv.at[here, k], m1_ssem, m1_rsem
        if n is None:
            n = k
        else:
            columns = pl.ds(pl.multiple_of(n * short, short), short)
            send, recv, n = send.at[:, columns], recv.at[:, columns], k + n
        return pltpu.make_async_remote_copy(
            src_ref=send, dst_ref=recv, send_sem=ssem.at[side, n], recv_sem=rsem.at[here, n],
            device_id=(px, py, sides[side]), device_id_type=MESH,
        )

    def columns(k, at):
        return pl.ds(pl.multiple_of(lax.rem(k, pieces) * span + at, 128), tile)

    def transform(rows, k, at):
        return jnp.dot(rows, snap[k // pieces, :, columns(k, at)], preferred_element_type=f32)

    def loaded(k):
        @pl.when(lax.rem(k, pieces) == 0)
        def _():
            load(k // pieces).wait()

    def tiles(width):
        def run(body):
            @pl.loop(0, width // tile)
            def _(i):
                body(pl.multiple_of(i * tile, tile))
        return run

    def meet(k):
        @pl.when(k == 0)
        def _():
            pl.semaphore_wait(barrier, len(sides) + len(peers))

    def finish(k, at, both):
        here = columns(k, at)
        weight = root[:, here]
        (r0, i0), (r1, i1) = parts = [
            (both[b * unit:b * unit + modes] * weight, both[b * unit + modes:(b + 1) * unit] * weight)
            for b in range(SEGMENT_NUMBER)]
        terms = (r0 * r0 + i0 * i0, r1 * r1 + i1 * i1, r0 * r1 + i0 * i1, r0 * i1 - i0 * r1)
        for n, term in enumerate(terms):
            lanes = [term[:, c:c + 128] for c in range(0, tile, 128)]
            acc[n] += functools.reduce(jnp.add, lanes)
        for block, pair in enumerate(parts):
            for c in range(2):
                out_ref[:, block, k // pieces, c, here] = pair[c]

    def weights():
        weight_copy.wait()
        root[...] = jnp.sqrt(weight_ref[...])

    @pl.when(inner)
    def _():
        @pl.loop(0, steps)
        def _(k):
            loaded(k)
            for side in range(2):
                @tiles(half)
                def _(at):
                    a_send[side, k, :, pl.ds(at, tile)] = transform(
                        twiddle[0:2 * unit, :], k, side * half + at).astype(bf16)
                if side == 0:
                    meet(k)
                remote(*a_refs, side, k).start()

        @pl.loop(0, steps)
        def _(k):
            for dependent in range(2):
                first = half * (me if dependent else 1 - me)
                if dependent:
                    for side in range(2):
                        landed(*n2_refs, side, k).wait_recv()

                @tiles(half)
                def _(at):
                    product = transform(twiddle[2 * unit:6 * unit, :], k, first + at)
                    there = pl.ds(pl.multiple_of(first + at, 128), tile)
                    for side in range(2):
                        for block in range(SEGMENT_NUMBER):
                            r = (side * SEGMENT_NUMBER + block) * unit
                            rows = product[r:r + unit]
                            if dependent and block != side:
                                rows = rows + n2_recv[block, k, :, pl.ds(at, tile)].astype(f32)
                            m1_send[side, k, block * unit:(block + 1) * unit, there] = rows.astype(bf16)

            @pl.when(k < steps - 1)
            def _():
                for side in range(2):
                    m1_copy(me, side, k).start()

            @pl.when(k == steps - 1)
            def _():
                for n in range(tail):
                    for side in range(2):
                        m1_copy(me, side, k, n).start()

        weights()

        @pl.loop(0, steps)
        def _(k):
            for side in range(2):
                landed(*a_refs, side, k).wait_recv()
                landed(*n1_refs, side, k).wait_recv()

            for side in range(2):
                @tiles(half)
                def _(at):
                    both = transform(own[...], k, side * half + at)
                    both = both + a_recv[side, k, :, pl.ds(at, tile)].astype(f32)
                    extra = n1_recv[1 - side, k, :, pl.ds(at, tile)].astype(f32)
                    rows = [both[:unit], both[unit:]]
                    rows[1 - side] = rows[1 - side] + extra
                    finish(k, side * half + at, jnp.concatenate(rows, axis=0))

    @pl.when(outer)
    def _():
        base = me * (3 * unit)
        far = pl.ds(pl.multiple_of(base, unit), unit)
        near = pl.ds(pl.multiple_of(base + unit, unit), 2 * unit)

        @pl.loop(0, steps)
        def _(k):
            loaded(k)
            for side in range(2):
                @tiles(half)
                def _(at):
                    n2_send[side, k, :, pl.ds(at, tile)] = transform(
                        twiddle[far, :], k, side * half + at).astype(bf16)
                if side == 0:
                    meet(k)
                remote(*n2_refs, side, k).start()

        @pl.loop(0, steps)
        def _(k):
            @tiles(half)
            def _(at):
                product = transform(twiddle[near, :], k, (1 - me) * half + at)
                for side in range(2):
                    n1_send[side, k, :, pl.ds(at, tile)] = product[side * unit:(side + 1) * unit].astype(bf16)
            for side in range(2):
                remote(*n1_refs, side, k).start()
            for side in range(2):
                landed(*a_refs, side, k).wait_recv()

            @tiles(half)
            def _(at):
                here = pl.ds(at, tile)
                product = transform(twiddle[near, :], k, me * half + at)
                for side in range(2):
                    rows = product[side * unit:(side + 1) * unit]
                    for block in range(SEGMENT_NUMBER):
                        there = slice(block * unit, (block + 1) * unit)
                        came = a_recv[1 - side, k, there, here].astype(f32)
                        total = came + jnp.where(me == block, rows, 0.0)
                        a_send[side, k, there, here] = total.astype(bf16)
            for side in range(2):
                remote(*a_refs, side, k).start()

        weights()

        def arrived(k, at):
            there = pl.ds(at, tile)
            both = transform(own[...], k, at)
            finish(k, at, both + (
                m1_recv[0, k, :, there].astype(f32) + m1_recv[1, k, :, there].astype(f32)))

        @pl.loop(0, steps - 1)
        def _(k):
            for side in range(2):
                m1_copy(side, side, k).wait_recv()
            tiles(span)(functools.partial(arrived, k))

        @pl.loop(0, tail)
        def _(n):
            for side in range(2):
                m1_copy(side, side, steps - 1, n).wait_recv()
            tiles(short)(lambda at: arrived(steps - 1, pl.multiple_of(n * short + at, tile)))

    lane = lax.broadcasted_iota(jnp.int32, gram_send.shape, 1)
    sums = jnp.zeros(gram_send.shape, f32)
    for n in range(4):
        sums = jnp.where(lane == n, jnp.sum(acc[n], axis=1, keepdims=True), sums)
    gram_send[...] = sums

    def gram_copy(n):
        i, j, x, y = peers[n]
        return pltpu.make_async_remote_copy(
            src_ref=gram_send, dst_ref=gram_recv.at[n],
            send_sem=gram_ssem.at[n], recv_sem=gram_rsem.at[n],
            device_id=(x, y, ta), device_id_type=MESH,
        )

    for n in range(len(peers)):
        gram_copy(n).start()

    @pl.when(inner)
    def _():
        @pl.loop(0, steps)
        def _(k):
            for side in range(2):
                remote(*a_refs, side, k).wait_send()

                @pl.when(k < steps - 1)
                def _():
                    m1_copy(me, side, k).wait_send()

        @pl.loop(0, tail)
        def _(n):
            for side in range(2):
                m1_copy(me, side, steps - 1, n).wait_send()

    @pl.when(outer)
    def _():
        @pl.loop(0, steps)
        def _(k):
            for side in range(2):
                for refs in (a_refs, n1_refs, n2_refs):
                    remote(*refs, side, k).wait_send()

    total = sums
    for n in range(len(peers)):
        gram_copy(n).wait()
        total = total + gram_recv[n]
    row = lax.broadcasted_iota(jnp.int32, (8, 128), 0)
    lane = lax.broadcasted_iota(jnp.int32, (8, 128), 1)
    pick = jnp.zeros((8, 128), f32)
    for r, n, sign in ((0, 0, 1.0), (2, 2, 1.0), (3, 3, 1.0), (4, 2, 1.0), (5, 3, -1.0), (6, 1, 1.0)):
        pick = jnp.where((row == r) & (lane == n), sign, pick)
    gram_ref[...] = gram_scale * lax.dot_general(
        pick, total, (((1,), (1,)), ((), ())),
        precision=lax.Precision.HIGHEST, preferred_element_type=f32,
    )


def flush_kernel(spectra, gram, spectra_out, gram_out, sems):
    copies = [pltpu.make_async_copy(gram, gram_out, sems.at[0])]
    for f in range(spectra.shape[0]):
        copies.append(pltpu.make_async_copy(spectra.at[f], spectra_out.at[f], sems.at[f + 1]))
    for copy in copies:
        copy.start()
    for copy in copies:
        copy.wait()


def kernel_on_device(snapshots, quad_weights, spectral_indices):
    record, variables, points = snapshots.shape
    groups = lax.axis_size("ta")
    npx, npy = lax.axis_size("px"), lax.axis_size("py")
    modes = spectral_indices.shape[0] // groups
    unit = 2 * modes
    pieces, tail = 2, 4
    span = points // pieces
    half = span // 2
    tile = math.gcd(512, span // tail)
    steps = variables * pieces
    bf16, f32 = jnp.bfloat16, jnp.float32
    peers = npx * npy - 1
    dma = pltpu.SemaphoreType.DMA
    hbm = pl.BlockSpec(memory_space=pltpu.HBM)
    vmem = pl.BlockSpec(memory_space=pltpu.VMEM)
    spectra, gram = pl.pallas_call(
        functools.partial(
            window_kernel, pieces, tail, tile, 1.0 / (points * npx * npy * variables)),
        out_shape=(
            jax.ShapeDtypeStruct((modes, SEGMENT_NUMBER, variables, 2, points), f32),
            jax.ShapeDtypeStruct((SEGMENT_NUMBER * SEGMENT_NUMBER * 2, modes), f32),
        ),
        in_specs=[hbm, hbm, hbm],
        out_specs=(vmem, vmem),
        scratch_shapes=[
            pltpu.VMEM((variables, record, points), bf16),
            pltpu.SMEM(spectral_indices.shape, jnp.int32),
            pltpu.VMEM((1, points), f32),
            pltpu.VMEM((3 * SEGMENT_NUMBER * unit, record), bf16),
            pltpu.VMEM((SEGMENT_NUMBER * unit, record), bf16),
            pltpu.VMEM((1, points), f32),
            pltpu.VMEM((2, steps, SEGMENT_NUMBER * unit, half), bf16),
            pltpu.VMEM((2, steps, SEGMENT_NUMBER * unit, half), bf16),
            pltpu.VMEM((2, steps, unit, half), bf16),
            pltpu.VMEM((2, steps, unit, half), bf16),
            pltpu.VMEM((2, steps, unit, half), bf16),
            pltpu.VMEM((2, steps, unit, half), bf16),
            pltpu.VMEM((2, steps, SEGMENT_NUMBER * unit, span), bf16),
            pltpu.VMEM((2, steps, SEGMENT_NUMBER * unit, span), bf16),
            pltpu.VMEM((4, modes, 128), f32),
            pltpu.VMEM((modes, 128), f32),
            pltpu.VMEM((peers, modes, 128), f32),
            dma((variables,)), dma, dma,
            dma((2, steps)), dma((2, steps)), dma((2, steps)), dma((2, steps)),
            dma((2, steps)), dma((2, steps)),
            dma((2, steps - 1 + tail)), dma((2, steps - 1 + tail)),
            dma((peers,)), dma((peers,)),
        ],
        compiler_params=pltpu.CompilerParams(
            collective_id=0, has_side_effects=True, vmem_limit_bytes=44 * 1024 * 1024),
        name="window_transform",
    )(*(
        pltpu.with_memory_space_constraint(a, pltpu.HBM)
        for a in (snapshots.transpose(1, 0, 2), quad_weights.reshape(1, points), spectral_indices)
    ))
    spectra, gram = pl.pallas_call(
        flush_kernel,
        out_shape=(
            jax.ShapeDtypeStruct(spectra.shape, f32), jax.ShapeDtypeStruct(gram.shape, f32)),
        in_specs=[vmem, vmem],
        out_specs=(hbm, hbm),
        scratch_shapes=[dma((modes + 1,))],
        compiler_params=pltpu.CompilerParams(vmem_limit_bytes=1024 * 1024),
        name="flush",
    )(*(pltpu.with_memory_space_constraint(a, pltpu.VMEM) for a in (spectra, gram)))
    gram = gram.reshape(SEGMENT_NUMBER, SEGMENT_NUMBER, 2, modes)
    return spectra.transpose(0, 1, 3, 2, 4), gram.transpose(3, 0, 1, 2)


def solution(mesh):
    square = mesh.shape["ta"] == 4
    return jax.shard_map(
        kernel_on_device if square else plain_on_device,
        mesh=mesh,
        in_specs=(P("ta", None, ("px", "py")), P(("px", "py")), P()),
        out_specs=(P("ta", None, None, None, ("px", "py")), P("ta", None, None, None)),
        check_vma=False,
    )
```

profile of v0, /device:TPU:0, one launch (start us, length us, event | category | flops | bytes accessed | tf_op | source)
XLA Modules:
  0.0 100.5 jit_solution(1272576083644829373)
XLA Ops:
  0.6 97.5 %window_transform.1 = (f32[8,2,5,2,8192]{4,3,2,1,0:T(2,128)S(1)}, f32[8,8]{1,0:T(8,128)S(1)}) custom-call(bf16[5,96,8192]{2,1,0:T(8,128)(2,1)} %bitcast.6, f32[1,8192]{1,0:T(1,128)} %bitcast.7, s32[32]{0:T(128)} %index_hbm.1), custom_call_target="tpu_custom_call" | custom-call | tf_op jit(solution)/shard_map/window_transform/pallas_call | solution.py:433
  98.1 2.4 %flush.1 = (f32[8,2,5,2,8192]{4,3,2,1,0:T(2,128)}, f32[8,8]{1,0:T(8,128)}) custom-call(f32[8,2,5,2,8192]{4,3,2,1,0:T(2,128)S(1)} %get-tuple-element.6.spectra, f32[8,8]{1,0:T(8,128)S(1)} %get-tuple-element.7.gram), custom_call_target="tpu_custom_call" | custom-call | tf_op jit(solution)/shard_map/flush/pallas_call | solution.py:473
where the time goes:
time: 101 us
  Pallas kernels  99.9 us (99%)
    pallas_call x1, Pallas kernels, kernel_on_device(): pl.pallas_call(functools.partial(window_kernel, pieces, tail, tile, 1.0 /...  97.5 us
    pallas_call x1, Pallas kernels, kernel_on_device(): pl.pallas_call(flush_kernel, out_shape=(jax.ShapeDtypeStruct(spectra.shap...  2.43 us

commit v1 on v0

--- a/solution.py
+++ b/solution.py
@@ -82,10 +82,10 @@
     snap_hbm, weight_hbm, index_hbm, out_ref, gram_ref,
     snap, index_ref, weight_ref, twiddle, own, root,
     a_send, a_recv, n1_send, n1_recv, n2_send, n2_recv, m1_send, m1_recv,
-    acc, gram_send, gram_recv,
+    p_send, p_recv, pre, e_send, e_recv, acc, gram_send, gram_recv,
     load_sem, index_sem, weight_sem,
     a_ssem, a_rsem, n1_ssem, n1_rsem, n2_ssem, n2_rsem, m1_ssem, m1_rsem,
-    gram_ssem, gram_rsem,
+    p_ssem, p_rsem, e_ssem, e_rsem, gram_ssem, gram_rsem,
 ):
     px, py, ta = lax.axis_index("px"), lax.axis_index("py"), lax.axis_index("ta")
     npx, npy = lax.axis_size("px"), lax.axis_size("py")
@@ -96,6 +96,7 @@
     span = points // pieces
     half = span // 2
     short = span // tail
+    common = steps - 2
     f32, bf16 = jnp.float32, jnp.bfloat16
 
     inner = (ta == 1) | (ta == 2)
@@ -103,12 +104,15 @@
     me = jnp.where(inner, ta - 1, ta // 3)
     sides = (jnp.where(inner, 0, 1), jnp.where(inner, 3, 2))
 
-    def load(variable):
-        return pltpu.make_async_copy(snap_hbm.at[variable], snap.at[variable], load_sem.at[variable])
+    def load(k):
+        there = pl.ds(pl.multiple_of(lax.rem(k, pieces) * span, span), span)
+        return pltpu.make_async_copy(
+            snap_hbm.at[k // pieces, :, there], snap.at[k // pieces, :, there], load_sem.at[k])
 
     index_copy = pltpu.make_async_copy(index_hbm, index_ref, index_sem)
     weight_copy = pltpu.make_async_copy(weight_hbm, weight_ref, weight_sem)
     index_copy.start()
+    load(0).start()
 
     peers = [
         (i, j, lax.rem(px + i, npx), lax.rem(py + j, npy))
@@ -119,10 +123,6 @@
         pl.semaphore_signal(barrier, inc=1, device_id=(px, py, side), device_id_type=MESH)
     for _, _, x, y in peers:
         pl.semaphore_signal(barrier, inc=1, device_id=(x, y, ta), device_id_type=MESH)
-
-    for variable in range(variables):
-        load(variable).start()
-    weight_copy.start()
 
     sublane = lax.broadcasted_iota(jnp.int32, (modes, record), 0)
     moment = lax.broadcasted_iota(jnp.int32, (modes, record), 1) + ta * record
@@ -174,12 +174,22 @@
             n = k
         else:
             columns = pl.ds(pl.multiple_of(n * short, short), short)
-            send, recv, n = send.at[:, columns], recv.at[:, columns], k + n
+            send, recv, n = send.at[:, columns], recv.at[:, columns], steps + n
         return pltpu.make_async_remote_copy(
             src_ref=send, dst_ref=recv, send_sem=ssem.at[side, n], recv_sem=rsem.at[here, n],
             device_id=(px, py, sides[side]), device_id_type=MESH,
         )
 
+    def lone_copy(send, recv, ssem, rsem, here, side):
+        return pltpu.make_async_remote_copy(
+            src_ref=send.at[side], dst_ref=recv.at[here],
+            send_sem=ssem.at[side], recv_sem=rsem.at[here],
+            device_id=(px, py, sides[side]), device_id_type=MESH,
+        )
+
+    p_refs = (p_send, p_recv, p_ssem, p_rsem)
+    e_refs = (e_send, e_recv, e_ssem, e_rsem)
+
     def columns(k, at):
         return pl.ds(pl.multiple_of(lax.rem(k, pieces) * span + at, 128), tile)
 
@@ -187,9 +197,13 @@
         return jnp.dot(rows, snap[k // pieces, :, columns(k, at)], preferred_element_type=f32)
 
     def loaded(k):
-        @pl.when(lax.rem(k, pieces) == 0)
+        load(k).wait()
+
+        @pl.when(k == 0)
         def _():
-            load(k // pieces).wait()
+            for later in range(1, steps):
+                load(later).start()
+            weight_copy.start()
 
     def tiles(width):
         def run(body):
@@ -203,23 +217,63 @@
         def _():
             pl.semaphore_wait(barrier, len(sides) + len(peers))
 
-    def finish(k, at, both):
-        here = columns(k, at)
-        weight = root[:, here]
-        (r0, i0), (r1, i1) = parts = [
+    def weighted(k, at, both):
+        weight = root[:, columns(k, at)]
+        return [
             (both[b * unit:b * unit + modes] * weight, both[b * unit + modes:(b + 1) * unit] * weight)
             for b in range(SEGMENT_NUMBER)]
+
+    def add_terms(place, parts):
+        (r0, i0), (r1, i1) = parts
         terms = (r0 * r0 + i0 * i0, r1 * r1 + i1 * i1, r0 * r1 + i0 * i1, r0 * i1 - i0 * r1)
         for n, term in enumerate(terms):
             lanes = [term[:, c:c + 128] for c in range(0, tile, 128)]
-            acc[n] += functools.reduce(jnp.add, lanes)
+            acc[place, n] += functools.reduce(jnp.add, lanes)
+
+    def store(k, at, parts):
+        here = columns(k, at)
         for block, pair in enumerate(parts):
             for c in range(2):
                 out_ref[:, block, k // pieces, c, here] = pair[c]
 
+    def sums_of(place):
+        lane = lax.broadcasted_iota(jnp.int32, gram_send.shape, 1)
+        sums = jnp.zeros(gram_send.shape, f32)
+        for n in range(4):
+            sums = jnp.where(lane == n, jnp.sum(acc[place, n], axis=1, keepdims=True), sums)
+        return sums
+
+    def gram_copy(n):
+        i, j, x, y = peers[n]
+        return pltpu.make_async_remote_copy(
+            src_ref=gram_send, dst_ref=gram_recv.at[n],
+            send_sem=gram_ssem.at[n], recv_sem=gram_rsem.at[n],
+            device_id=(x, y, ta), device_id_type=MESH,
+        )
+
+    def exchange(sums):
+        gram_send[...] = sums
+        for n in range(len(peers)):
+            gram_copy(n).start()
+
     def weights():
         weight_copy.wait()
         root[...] = jnp.sqrt(weight_ref[...])
+
+    def gather():
+        total = gram_send[...]
+        for n in range(len(peers)):
+            gram_copy(n).wait()
+            total = total + gram_recv[n]
+        row = lax.broadcasted_iota(jnp.int32, (8, 128), 0)
+        lane = lax.broadcasted_iota(jnp.int32, (8, 128), 1)
+        pick = jnp.zeros((8, 128), f32)
+        for r, n, sign in ((0, 0, 1.0), (2, 2, 1.0), (3, 3, 1.0), (4, 2, 1.0), (5, 3, -1.0), (6, 1, 1.0)):
+            pick = jnp.where((row == r) & (lane == n), sign, pick)
+        gram_ref[...] = gram_scale * lax.dot_general(
+            pick, total, (((1,), (1,)), ((), ())),
+            precision=lax.Precision.HIGHEST, preferred_element_type=f32,
+        )
 
     @pl.when(inner)
     def _():
@@ -236,7 +290,9 @@
                 remote(*a_refs, side, k).start()
 
         @pl.loop(0, steps)
-        def _(k):
+        def _(j):
+            last = j == steps - 1
+            k = jnp.where(j == 0, steps - 1 - me, jnp.where(last, common + me, j - 1))
             for dependent in range(2):
                 first = half * (me if dependent else 1 - me)
                 if dependent:
@@ -255,16 +311,10 @@
                                 rows = rows + n2_recv[block, k, :, pl.ds(at, tile)].astype(f32)
                             m1_send[side, k, block * unit:(block + 1) * unit, there] = rows.astype(bf16)
 
-            @pl.when(k < steps - 1)
+            @pl.when(jnp.logical_not(last))
             def _():
                 for side in range(2):
                     m1_copy(me, side, k).start()
-
-            @pl.when(k == steps - 1)
-            def _():
-                for n in range(tail):
-                    for side in range(2):
-                        m1_copy(me, side, k, n).start()
 
         weights()
 
@@ -282,7 +332,45 @@
                     extra = n1_recv[1 - side, k, :, pl.ds(at, tile)].astype(f32)
                     rows = [both[:unit], both[unit:]]
                     rows[1 - side] = rows[1 - side] + extra
-                    finish(k, side * half + at, jnp.concatenate(rows, axis=0))
+                    parts = weighted(k, side * half + at, jnp.concatenate(rows, axis=0))
+                    add_terms(0, parts)
+                    store(k, side * half + at, parts)
+
+        exchange(sums_of(0))
+        for side in range(2):
+            lone_copy(*p_refs, side, side).wait_recv()
+
+            @tiles(span)
+            def _(at):
+                there = pl.ds(at, tile)
+                k = common + me
+                both = p_recv[side, :, there].astype(f32) + m1_send[side, k, :, there].astype(f32)
+                add_terms(1 + side, weighted(k, at, both))
+
+            e_send[side] = sums_of(1 + side)
+            lone_copy(*e_refs, me, side).start()
+
+        for n in range(tail):
+            for side in range(2):
+                m1_copy(me, side, common + me, n).start()
+
+        gather()
+        for side in range(2):
+            lone_copy(*e_refs, me, side).wait_send()
+
+        @pl.loop(0, steps)
+        def _(k):
+            for side in range(2):
+                remote(*a_refs, side, k).wait_send()
+
+                @pl.when(k != common + me)
+                def _():
+                    m1_copy(me, side, k).wait_send()
+
+        @pl.loop(0, tail)
+        def _(n):
+            for side in range(2):
+                m1_copy(me, side, common + me, n).wait_send()
 
     @pl.when(outer)
     def _():
@@ -330,78 +418,66 @@
 
         weights()
 
+        for side in range(2):
+            k = common + side
+            m1_copy(1 - side, 1 - side, k).wait_recv()
+
+            @tiles(span)
+            def _(at):
+                there = pl.ds(at, tile)
+                both = transform(own[...], k, at) + m1_recv[1 - side, k, :, there].astype(f32)
+                p_send[side, :, there] = both.astype(bf16)
+                pre[side, :, there] = both
+
+            lone_copy(*p_refs, me, side).start()
+
         def arrived(k, at):
             there = pl.ds(at, tile)
             both = transform(own[...], k, at)
-            finish(k, at, both + (
+            return weighted(k, at, both + (
                 m1_recv[0, k, :, there].astype(f32) + m1_recv[1, k, :, there].astype(f32)))
 
-        @pl.loop(0, steps - 1)
+        @pl.loop(0, common)
         def _(k):
             for side in range(2):
                 m1_copy(side, side, k).wait_recv()
-            tiles(span)(functools.partial(arrived, k))
+
+            @tiles(span)
+            def _(at):
+                parts = arrived(k, at)
+                add_terms(0, parts)
+                store(k, at, parts)
+
+        sums = sums_of(0)
+        for side in range(2):
+            lone_copy(*e_refs, side, side).wait_recv()
+            sums = sums + e_recv[side]
+        exchange(sums)
+
+        @pl.loop(0, steps)
+        def _(k):
+            for side in range(2):
+                for refs in (a_refs, n1_refs, n2_refs):
+                    remote(*refs, side, k).wait_send()
+
+        for side in range(2):
+            lone_copy(*p_refs, me, side).wait_send()
 
         @pl.loop(0, tail)
         def _(n):
-            for side in range(2):
-                m1_copy(side, side, steps - 1, n).wait_recv()
-            tiles(short)(lambda at: arrived(steps - 1, pl.multiple_of(n * short + at, tile)))
-
-    lane = lax.broadcasted_iota(jnp.int32, gram_send.shape, 1)
-    sums = jnp.zeros(gram_send.shape, f32)
-    for n in range(4):
-        sums = jnp.where(lane == n, jnp.sum(acc[n], axis=1, keepdims=True), sums)
-    gram_send[...] = sums
-
-    def gram_copy(n):
-        i, j, x, y = peers[n]
-        return pltpu.make_async_remote_copy(
-            src_ref=gram_send, dst_ref=gram_recv.at[n],
-            send_sem=gram_ssem.at[n], recv_sem=gram_rsem.at[n],
-            device_id=(x, y, ta), device_id_type=MESH,
-        )
-
-    for n in range(len(peers)):
-        gram_copy(n).start()
-
-    @pl.when(inner)
-    def _():
-        @pl.loop(0, steps)
-        def _(k):
-            for side in range(2):
-                remote(*a_refs, side, k).wait_send()
-
-                @pl.when(k < steps - 1)
-                def _():
-                    m1_copy(me, side, k).wait_send()
-
-        @pl.loop(0, tail)
-        def _(n):
-            for side in range(2):
-                m1_copy(me, side, steps - 1, n).wait_send()
-
-    @pl.when(outer)
-    def _():
-        @pl.loop(0, steps)
-        def _(k):
-            for side in range(2):
-                for refs in (a_refs, n1_refs, n2_refs):
-                    remote(*refs, side, k).wait_send()
-
-    total = sums
-    for n in range(len(peers)):
-        gram_copy(n).wait()
-        total = total + gram_recv[n]
-    row = lax.broadcasted_iota(jnp.int32, (8, 128), 0)
-    lane = lax.broadcasted_iota(jnp.int32, (8, 128), 1)
-    pick = jnp.zeros((8, 128), f32)
-    for r, n, sign in ((0, 0, 1.0), (2, 2, 1.0), (3, 3, 1.0), (4, 2, 1.0), (5, 3, -1.0), (6, 1, 1.0)):
-        pick = jnp.where((row == r) & (lane == n), sign, pick)
-    gram_ref[...] = gram_scale * lax.dot_general(
-        pick, total, (((1,), (1,)), ((), ())),
-        precision=lax.Precision.HIGHEST, preferred_element_type=f32,
-    )
+            @pl.when(n == tail - 1)
+            def _():
+                gather()
+
+            for side in range(2):
+                k = common + side
+                m1_copy(side, side, k, n).wait_recv()
+
+                for c in range(0, short, tile):
+                    at = pl.multiple_of(n * short + c, tile)
+                    there = pl.ds(at, tile)
+                    store(k, at, weighted(
+                        k, at, pre[side, :, there] + m1_recv[side, k, :, there].astype(f32)))
 
 
 def flush_kernel(spectra, gram, spectra_out, gram_out, sems):
@@ -454,13 +530,19 @@
             pltpu.VMEM((2, steps, unit, half), bf16),
             pltpu.VMEM((2, steps, SEGMENT_NUMBER * unit, span), bf16),
             pltpu.VMEM((2, steps, SEGMENT_NUMBER * unit, span), bf16),
-            pltpu.VMEM((4, modes, 128), f32),
+            pltpu.VMEM((2, SEGMENT_NUMBER * unit, span), bf16),
+            pltpu.VMEM((2, SEGMENT_NUMBER * unit, span), bf16),
+            pltpu.VMEM((2, SEGMENT_NUMBER * unit, span), f32),
+            pltpu.VMEM((2, modes, 128), f32),
+            pltpu.VMEM((2, modes, 128), f32),
+            pltpu.VMEM((3, 4, modes, 128), f32),
             pltpu.VMEM((modes, 128), f32),
             pltpu.VMEM((peers, modes, 128), f32),
-            dma((variables,)), dma, dma,
+            dma((steps,)), dma, dma,
             dma((2, steps)), dma((2, steps)), dma((2, steps)), dma((2, steps)),
             dma((2, steps)), dma((2, steps)),
-            dma((2, steps - 1 + tail)), dma((2, steps - 1 + tail)),
+            dma((2, steps + tail)), dma((2, steps + tail)),
+            dma((2,)), dma((2,)), dma((2,)), dma((2,)),
             dma((peers,)), dma((peers,)),
         ],
         compiler_params=pltpu.CompilerParams(

time: 101 us -> 97.2 us (0.962)
  Pallas kernels: 99.9 us -> 96.4 us
    pallas_call x1, Pallas kernels: 97.5 us -> 94 us  [kernel_on_device(): pl.pallas_call(functools.partial(window_kernel, pieces, tail, tile, 1.0 /...]
where the time goes in v1:
time: 97.2 us; the launch traced here: 97 us
  Pallas kernels  96.4 us (99%)
    pallas_call x1, Pallas kernels, kernel_on_device(): pl.pallas_call(functools.partial(window_kernel, pieces, tail, tile, 1.0 /...  94 us
    pallas_call x1, Pallas kernels, kernel_on_device(): pl.pallas_call(flush_kernel, out_shape=(jax.ShapeDtypeStruct(spectra.shap...  2.43 us

profile of v1, /device:TPU:0, one launch (start us, length us, event | category | flops | bytes accessed | tf_op | source)
XLA Modules:
  0.0 97.0 jit_solution(1330222777945711765)
XLA Ops:
  0.6 94.0 %window_transform.1 = (f32[8,2,5,2,8192]{4,3,2,1,0:T(2,128)S(1)}, f32[8,8]{1,0:T(8,128)S(1)}) custom-call(bf16[5,96,8192]{2,1,0:T(8,128)(2,1)} %bitcast.6, f32[1,8192]{1,0:T(1,128)} %bitcast.7, s32[32]{0:T(128)} %index_hbm.1), custom_call_target="tpu_custom_call" | custom-call | tf_op jit(solution)/shard_map/window_transform/pallas_call | solution.py:509
  94.6 2.4 %flush.1 = (f32[8,2,5,2,8192]{4,3,2,1,0:T(2,128)}, f32[8,8]{1,0:T(8,128)}) custom-call(f32[8,2,5,2,8192]{4,3,2,1,0:T(2,128)S(1)} %get-tuple-element.6.spectra, f32[8,8]{1,0:T(8,128)S(1)} %get-tuple-element.7.gram), custom_call_target="tpu_custom_call" | custom-call | tf_op jit(solution)/shard_map/flush/pallas_call | solution.py:555

commit v2 on v1

--- a/solution.py
+++ b/solution.py
@@ -85,7 +85,7 @@
     p_send, p_recv, pre, e_send, e_recv, acc, gram_send, gram_recv,
     load_sem, index_sem, weight_sem,
     a_ssem, a_rsem, n1_ssem, n1_rsem, n2_ssem, n2_rsem, m1_ssem, m1_rsem,
-    p_ssem, p_rsem, e_ssem, e_rsem, gram_ssem, gram_rsem,
+    p_ssem, p_rsem, e_ssem, e_rsem, gram_ssem, gram_rsem, ready_sem,
 ):
     px, py, ta = lax.axis_index("px"), lax.axis_index("py"), lax.axis_index("ta")
     npx, npy = lax.axis_size("px"), lax.axis_size("py")
@@ -121,8 +121,14 @@
     barrier = pltpu.get_barrier_semaphore()
     for side in sides:
         pl.semaphore_signal(barrier, inc=1, device_id=(px, py, side), device_id_type=MESH)
-    for _, _, x, y in peers:
-        pl.semaphore_signal(barrier, inc=1, device_id=(x, y, ta), device_id_type=MESH)
+    for i in range(1, npx):
+        pl.semaphore_signal(barrier, inc=1, device_id=(lax.rem(px + i, npx), py, ta), device_id_type=MESH)
+    below, above = py > 0, py < npy - 1
+    for there, step in ((below, -1), (above, 1)):
+        @pl.when(there)
+        def _():
+            pl.semaphore_signal(barrier, inc=1, device_id=(px, py + step, ta), device_id_type=MESH)
+    greeted = len(sides) + npx - 1 + jnp.where(below, 1, 0) + jnp.where(above, 1, 0)
 
     sublane = lax.broadcasted_iota(jnp.int32, (modes, record), 0)
     moment = lax.broadcasted_iota(jnp.int32, (modes, record), 1) + ta * record
@@ -205,9 +211,9 @@
                 load(later).start()
             weight_copy.start()
 
-    def tiles(width):
+    def tiles(width, unroll=1):
         def run(body):
-            @pl.loop(0, width // tile)
+            @pl.loop(0, width // tile, unroll=unroll)
             def _(i):
                 body(pl.multiple_of(i * tile, tile))
         return run
@@ -215,7 +221,24 @@
     def meet(k):
         @pl.when(k == 0)
         def _():
-            pl.semaphore_wait(barrier, len(sides) + len(peers))
+            pl.semaphore_wait(barrier, greeted)
+
+    def learn_of_peers():
+        for n, (back, forth, step) in enumerate(((below, above, 1), (above, below, -1))):
+            @pl.when(back)
+            def _():
+                pl.semaphore_wait(ready_sem.at[n], 1)
+
+            @pl.when(forth)
+            def _():
+                pl.semaphore_signal(
+                    ready_sem.at[n], inc=1, device_id=(px, py + step, ta), device_id_type=MESH)
+
+        for i in range(1, npx):
+            pl.semaphore_signal(
+                ready_sem.at[2], inc=1, device_id=(lax.rem(px + i, npx), py, ta), device_id_type=MESH)
+        if npx > 1:
+            pl.semaphore_wait(ready_sem.at[2], npx - 1)
 
     def weighted(k, at, both):
         weight = root[:, columns(k, at)]
@@ -281,7 +304,7 @@
         def _(k):
             loaded(k)
             for side in range(2):
-                @tiles(half)
+                @tiles(half, 4)
                 def _(at):
                     a_send[side, k, :, pl.ds(at, tile)] = transform(
                         twiddle[0:2 * unit, :], k, side * half + at).astype(bf16)
@@ -317,6 +340,7 @@
                     m1_copy(me, side, k).start()
 
         weights()
+        learn_of_peers()
 
         @pl.loop(0, steps)
         def _(k):
@@ -382,7 +406,7 @@
         def _(k):
             loaded(k)
             for side in range(2):
-                @tiles(half)
+                @tiles(half, 4)
                 def _(at):
                     n2_send[side, k, :, pl.ds(at, tile)] = transform(
                         twiddle[far, :], k, side * half + at).astype(bf16)
@@ -431,6 +455,8 @@
 
             lone_copy(*p_refs, me, side).start()
 
+        learn_of_peers()
+
         def arrived(k, at):
             there = pl.ds(at, tile)
             both = transform(own[...], k, at)
@@ -442,7 +468,7 @@
             for side in range(2):
                 m1_copy(side, side, k).wait_recv()
 
-            @tiles(span)
+            @tiles(span, 2)
             def _(at):
                 parts = arrived(k, at)
                 add_terms(0, parts)
@@ -544,6 +570,7 @@
             dma((2, steps + tail)), dma((2, steps + tail)),
             dma((2,)), dma((2,)), dma((2,)), dma((2,)),
             dma((peers,)), dma((peers,)),
+            pltpu.SemaphoreType.REGULAR((3,)),
         ],
         compiler_params=pltpu.CompilerParams(
             collective_id=0, has_side_effects=True, vmem_limit_bytes=44 * 1024 * 1024),

time: 97.2 us -> 96.2 us (0.990)
  Pallas kernels: 96.4 us -> 95.4 us
    pallas_call x1, Pallas kernels: 94 us -> 93 us  [kernel_on_device(): pl.pallas_call(functools.partial(window_kernel, pieces, tail, tile, 1.0 /...]
where the time goes in v2:
time: 96.2 us; the launch traced here: 96 us
  Pallas kernels  95.4 us (99%)
    pallas_call x1, Pallas kernels, kernel_on_device(): pl.pallas_call(functools.partial(window_kernel, pieces, tail, tile, 1.0 /...  93 us
    pallas_call x1, Pallas kernels, kernel_on_device(): pl.pallas_call(flush_kernel, out_shape=(jax.ShapeDtypeStruct(spectra.shap...  2.43 us

profile of v2, /device:TPU:0, one launch (start us, length us, event | category | flops | bytes accessed | tf_op | source)
XLA Modules:
  0.0 96.0 jit_solution(9786396216753215347)
XLA Ops:
  0.6 93.0 %window_transform.1 = (f32[8,2,5,2,8192]{4,3,2,1,0:T(2,128)S(1)}, f32[8,8]{1,0:T(8,128)S(1)}) custom-call(bf16[5,96,8192]{2,1,0:T(8,128)(2,1)} %bitcast.6, f32[1,8192]{1,0:T(1,128)} %bitcast.7, s32[32]{0:T(128)} %index_hbm.1), custom_call_target="tpu_custom_call" | custom-call | tf_op jit(solution)/shard_map/window_transform/pallas_call | solution.py:535
  93.6 2.4 %flush.1 = (f32[8,2,5,2,8192]{4,3,2,1,0:T(2,128)}, f32[8,8]{1,0:T(8,128)}) custom-call(f32[8,2,5,2,8192]{4,3,2,1,0:T(2,128)S(1)} %get-tuple-element.6.spectra, f32[8,8]{1,0:T(8,128)S(1)} %get-tuple-element.7.gram), custom_call_target="tpu_custom_call" | custom-call | tf_op jit(solution)/shard_map/flush/pallas_call | solution.py:582

commit v3 on v2

--- a/solution.py
+++ b/solution.py
@@ -82,9 +82,10 @@
     snap_hbm, weight_hbm, index_hbm, out_ref, gram_ref,
     snap, index_ref, weight_ref, twiddle, own, root,
     a_send, a_recv, n1_send, n1_recv, n2_send, n2_recv, m1_send, m1_recv,
-    p_send, p_recv, pre, e_send, e_recv, acc, gram_send, gram_recv,
+    relay, p_send, p_recv, pre, e_send, e_recv, acc, gram_send, gram_recv,
     load_sem, index_sem, weight_sem,
     a_ssem, a_rsem, n1_ssem, n1_rsem, n2_ssem, n2_rsem, m1_ssem, m1_rsem,
+    relay_ssem, relay_rsem, lift_ssem, lift_rsem,
     p_ssem, p_rsem, e_ssem, e_rsem, gram_ssem, gram_rsem, ready_sem,
 ):
     px, py, ta = lax.axis_index("px"), lax.axis_index("py"), lax.axis_index("ta")
@@ -96,7 +97,8 @@
     span = points // pieces
     half = span // 2
     short = span // tail
-    common = steps - 2
+    common = steps - 4
+    lifts, lift = relay.shape[0], relay.shape[3]
     f32, bf16 = jnp.float32, jnp.bfloat16
 
     inner = (ta == 1) | (ta == 2)
@@ -180,21 +182,64 @@
             n = k
         else:
             columns = pl.ds(pl.multiple_of(n * short, short), short)
-            send, recv, n = send.at[:, columns], recv.at[:, columns], steps + n
+            send, recv = send.at[:, columns], recv.at[:, columns]
+            n = steps + n + jnp.where(k == common - 1, tail, 0)
         return pltpu.make_async_remote_copy(
             src_ref=send, dst_ref=recv, send_sem=ssem.at[side, n], recv_sem=rsem.at[here, n],
             device_id=(px, py, sides[side]), device_id_type=MESH,
         )
 
-    def lone_copy(send, recv, ssem, rsem, here, side):
-        return pltpu.make_async_remote_copy(
-            src_ref=send.at[side], dst_ref=recv.at[here],
-            send_sem=ssem.at[side], recv_sem=rsem.at[here],
+    def lifted_copy(here, side, c):
+        columns = pl.ds(c * lift, lift)
+        return pltpu.make_async_remote_copy(
+            src_ref=m1_send.at[side, 0, :, columns], dst_ref=m1_recv.at[here, 0, :, columns],
+            send_sem=lift_ssem.at[c, side], recv_sem=lift_rsem.at[c, here],
             device_id=(px, py, sides[side]), device_id_type=MESH,
         )
 
-    p_refs = (p_send, p_recv, p_ssem, p_rsem)
-    e_refs = (e_send, e_recv, e_ssem, e_rsem)
+    def up_copy(here, side, c):
+        return pltpu.make_async_remote_copy(
+            src_ref=m1_send.at[side, 0, :, pl.ds(c * lift, lift)], dst_ref=relay.at[c, here],
+            send_sem=lift_ssem.at[c, side], recv_sem=relay_rsem.at[c, here],
+            device_id=(px, py + 1, sides[side]), device_id_type=MESH,
+        )
+
+    def down_copy(side, c):
+        return pltpu.make_async_remote_copy(
+            src_ref=relay.at[c, side], dst_ref=m1_recv.at[side, 0, :, pl.ds(c * lift, lift)],
+            send_sem=relay_ssem.at[c, side], recv_sem=lift_rsem.at[c, side],
+            device_id=(px, py - 1, ta), device_id_type=MESH,
+        )
+
+    def goes_up(c):
+        return c < npy - 1 - py
+
+    def comes_up(c):
+        return (py > 0) & (c < npy - py)
+
+    def rest_copy(here, side):
+        columns = pl.ds(lifts * lift, span - lifts * lift)
+        return pltpu.make_async_remote_copy(
+            src_ref=m1_send.at[side, 0, :, columns], dst_ref=m1_recv.at[here, 0, :, columns],
+            send_sem=m1_ssem.at[side, 0], recv_sem=m1_rsem.at[here, 0],
+            device_id=(px, py, sides[side]), device_id_type=MESH,
+        )
+
+    def p_copy(here, side, u):
+        return pltpu.make_async_remote_copy(
+            src_ref=p_send.at[side, u], dst_ref=p_recv.at[here, u],
+            send_sem=p_ssem.at[side, u], recv_sem=p_rsem.at[here, u],
+            device_id=(px, py, sides[side]), device_id_type=MESH,
+        )
+
+    beside = jnp.bitwise_xor(py, 1) if npy % 2 == 0 else py
+
+    def e_copy(here, side):
+        return pltpu.make_async_remote_copy(
+            src_ref=e_send.at[side], dst_ref=e_recv.at[here],
+            send_sem=e_ssem.at[side], recv_sem=e_rsem.at[here],
+            device_id=(px, beside, sides[side]), device_id_type=MESH,
+        )
 
     def columns(k, at):
         return pl.ds(pl.multiple_of(lax.rem(k, pieces) * span + at, 128), tile)
@@ -314,8 +359,9 @@
 
         @pl.loop(0, steps)
         def _(j):
-            last = j == steps - 1
-            k = jnp.where(j == 0, steps - 1 - me, jnp.where(last, common + me, j - 1))
+            k = jnp.where(
+                j < 2, common + 2 * j + 1 - me,
+                jnp.where(j < common + 2, j - 2, common + 2 * (j - common - 2) + me))
             for dependent in range(2):
                 first = half * (me if dependent else 1 - me)
                 if dependent:
@@ -334,10 +380,33 @@
                                 rows = rows + n2_recv[block, k, :, pl.ds(at, tile)].astype(f32)
                             m1_send[side, k, block * unit:(block + 1) * unit, there] = rows.astype(bf16)
 
-            @pl.when(jnp.logical_not(last))
+            split = (k == common - 1) | (j == steps - 1)
+
+            @pl.when(split)
+            def _():
+                for n in range(tail):
+                    for side in range(2):
+                        m1_copy(me, side, k, n).start()
+
+            @pl.when(k == 0)
+            def _():
+                for c in range(lifts):
+                    for side in range(2):
+                        @pl.when(goes_up(c))
+                        def _():
+                            up_copy(me, side, c).start()
+
+                        @pl.when(jnp.logical_not(goes_up(c)))
+                        def _():
+                            lifted_copy(me, side, c).start()
+                for side in range(2):
+                    rest_copy(me, side).start()
+
+            @pl.when(jnp.logical_not(split) & (k != 0))
             def _():
                 for side in range(2):
                     m1_copy(me, side, k).start()
+
 
         weights()
         learn_of_peers()
@@ -361,40 +430,44 @@
                     store(k, side * half + at, parts)
 
         exchange(sums_of(0))
+        for u in range(2):
+            for side in range(2):
+                p_copy(side, side, u).wait_recv()
+
+                @tiles(span, 2)
+                def _(at):
+                    there = pl.ds(at, tile)
+                    k = common + 2 * u + me
+                    both = p_recv[side, u, :, there].astype(f32) + m1_send[side, k, :, there].astype(f32)
+                    add_terms(1 + side, weighted(k, at, both))
+
         for side in range(2):
-            lone_copy(*p_refs, side, side).wait_recv()
-
-            @tiles(span)
-            def _(at):
-                there = pl.ds(at, tile)
-                k = common + me
-                both = p_recv[side, :, there].astype(f32) + m1_send[side, k, :, there].astype(f32)
-                add_terms(1 + side, weighted(k, at, both))
-
             e_send[side] = sums_of(1 + side)
-            lone_copy(*e_refs, me, side).start()
-
-        for n in range(tail):
-            for side in range(2):
-                m1_copy(me, side, common + me, n).start()
+            e_copy(me, side).start()
 
         gather()
         for side in range(2):
-            lone_copy(*e_refs, me, side).wait_send()
+            e_copy(me, side).wait_send()
 
         @pl.loop(0, steps)
         def _(k):
             for side in range(2):
                 remote(*a_refs, side, k).wait_send()
 
-                @pl.when(k != common + me)
+                @pl.when((k != common + 2 + me) & (k != common - 1) & (k > 0))
                 def _():
                     m1_copy(me, side, k).wait_send()
 
+        for side in range(2):
+            rest_copy(me, side).wait_send()
+            for c in range(lifts):
+                lifted_copy(me, side, c).wait_send()
+
         @pl.loop(0, tail)
         def _(n):
             for side in range(2):
-                m1_copy(me, side, common + me, n).wait_send()
+                m1_copy(me, side, common - 1, n).wait_send()
+                m1_copy(me, side, common + 2 + me, n).wait_send()
 
     @pl.when(outer)
     def _():
@@ -442,18 +515,26 @@
 
         weights()
 
-        for side in range(2):
-            k = common + side
-            m1_copy(1 - side, 1 - side, k).wait_recv()
-
-            @tiles(span)
-            def _(at):
-                there = pl.ds(at, tile)
-                both = transform(own[...], k, at) + m1_recv[1 - side, k, :, there].astype(f32)
-                p_send[side, :, there] = both.astype(bf16)
-                pre[side, :, there] = both
-
-            lone_copy(*p_refs, me, side).start()
+        for c in range(lifts):
+            @pl.when(comes_up(c))
+            def _():
+                for side in range(2):
+                    up_copy(side, side, c).wait_recv()
+                    down_copy(side, c).start()
+
+        for u in range(2):
+            for side in range(2):
+                k = common + 2 * u + side
+                m1_copy(1 - side, 1 - side, k).wait_recv()
+
+                @tiles(span, 2)
+                def _(at):
+                    there = pl.ds(at, tile)
+                    both = transform(own[...], k, at) + m1_recv[1 - side, k, :, there].astype(f32)
+                    p_send[side, u, :, there] = both.astype(bf16)
+                    pre[side, u, :, there] = both
+
+                p_copy(me, side, u).start()
 
         learn_of_peers()
 
@@ -463,20 +544,37 @@
             return weighted(k, at, both + (
                 m1_recv[0, k, :, there].astype(f32) + m1_recv[1, k, :, there].astype(f32)))
 
-        @pl.loop(0, common)
-        def _(k):
-            for side in range(2):
-                m1_copy(side, side, k).wait_recv()
-
-            @tiles(span, 2)
+        def arrive(k, first, width):
+            @tiles(width, 2)
             def _(at):
+                at = pl.multiple_of(first + at, tile)
                 parts = arrived(k, at)
                 add_terms(0, parts)
                 store(k, at, parts)
 
+        @pl.loop(0, common - 1)
+        def _(k):
+            for side in range(2):
+                @pl.when(k == 0)
+                def _():
+                    for c in range(lifts):
+                        lifted_copy(side, side, c).wait_recv()
+                    rest_copy(side, side).wait_recv()
+
+                @pl.when(k > 0)
+                def _():
+                    m1_copy(side, side, k).wait_recv()
+            arrive(k, 0, span)
+
+        @pl.loop(0, tail)
+        def _(n):
+            for side in range(2):
+                m1_copy(side, side, common - 1, n).wait_recv()
+            arrive(common - 1, n * short, short)
+
         sums = sums_of(0)
         for side in range(2):
-            lone_copy(*e_refs, side, side).wait_recv()
+            e_copy(side, side).wait_recv()
             sums = sums + e_recv[side]
         exchange(sums)
 
@@ -487,23 +585,35 @@
                     remote(*refs, side, k).wait_send()
 
         for side in range(2):
-            lone_copy(*p_refs, me, side).wait_send()
+            for u in range(2):
+                p_copy(me, side, u).wait_send()
+
+        for c in range(lifts):
+            @pl.when(comes_up(c))
+            def _():
+                for side in range(2):
+                    down_copy(side, c).wait_send()
+
+        def complete(side, u, at):
+            k = common + 2 * u + side
+            there = pl.ds(at, tile)
+            store(k, at, weighted(
+                k, at, pre[side, u, :, there] + m1_recv[side, k, :, there].astype(f32)))
+
+        for side in range(2):
+            m1_copy(side, side, common + side).wait_recv()
+            tiles(span, 2)(functools.partial(complete, side, 0))
 
         @pl.loop(0, tail)
         def _(n):
-            @pl.when(n == tail - 1)
+            @pl.when(n == tail // 2)
             def _():
                 gather()
 
             for side in range(2):
-                k = common + side
-                m1_copy(side, side, k, n).wait_recv()
-
+                m1_copy(side, side, common + 2 + side, n).wait_recv()
                 for c in range(0, short, tile):
-                    at = pl.multiple_of(n * short + c, tile)
-                    there = pl.ds(at, tile)
-                    store(k, at, weighted(
-                        k, at, pre[side, :, there] + m1_recv[side, k, :, there].astype(f32)))
+                    complete(side, 1, pl.multiple_of(n * short + c, tile))
 
 
 def flush_kernel(spectra, gram, spectra_out, gram_out, sems):
@@ -527,6 +637,8 @@
     half = span // 2
     tile = math.gcd(512, span // tail)
     steps = variables * pieces
+    lift = min(256, span // npy)
+    lifts = npy - 1
     bf16, f32 = jnp.bfloat16, jnp.float32
     peers = npx * npy - 1
     dma = pltpu.SemaphoreType.DMA
@@ -556,9 +668,10 @@
             pltpu.VMEM((2, steps, unit, half), bf16),
             pltpu.VMEM((2, steps, SEGMENT_NUMBER * unit, span), bf16),
             pltpu.VMEM((2, steps, SEGMENT_NUMBER * unit, span), bf16),
-            pltpu.VMEM((2, SEGMENT_NUMBER * unit, span), bf16),
-            pltpu.VMEM((2, SEGMENT_NUMBER * unit, span), bf16),
-            pltpu.VMEM((2, SEGMENT_NUMBER * unit, span), f32),
+            pltpu.VMEM((lifts, 2, SEGMENT_NUMBER * unit, lift), bf16),
+            pltpu.VMEM((2, 2, SEGMENT_NUMBER * unit, span), bf16),
+            pltpu.VMEM((2, 2, SEGMENT_NUMBER * unit, span), bf16),
+            pltpu.VMEM((2, 2, SEGMENT_NUMBER * unit, span), f32),
             pltpu.VMEM((2, modes, 128), f32),
             pltpu.VMEM((2, modes, 128), f32),
             pltpu.VMEM((3, 4, modes, 128), f32),
@@ -567,8 +680,9 @@
             dma((steps,)), dma, dma,
             dma((2, steps)), dma((2, steps)), dma((2, steps)), dma((2, steps)),
             dma((2, steps)), dma((2, steps)),
-            dma((2, steps + tail)), dma((2, steps + tail)),
-            dma((2,)), dma((2,)), dma((2,)), dma((2,)),
+            dma((2, steps + 2 * tail)), dma((2, steps + 2 * tail)),
+            dma((lifts, 2)), dma((lifts, 2)), dma((lifts, 2)), dma((lifts, 2)),
+            dma((2, 2)), dma((2, 2)), dma((2,)), dma((2,)),
             dma((peers,)), dma((peers,)),
             pltpu.SemaphoreType.REGULAR((3,)),
         ],

time: 96.2 us -> 93.9 us (0.976)
  Pallas kernels: 95.4 us -> 93.1 us
    pallas_call x1, Pallas kernels: 93 us -> 90.7 us  [kernel_on_device(): pl.pallas_call(functools.partial(window_kernel, pieces, tail, tile, 1.0 /...]
where the time goes in v3:
time: 93.9 us; the launch traced here: 93.8 us
  Pallas kernels  93.1 us (99%)
    pallas_call x1, Pallas kernels, kernel_on_device(): pl.pallas_call(functools.partial(window_kernel, pieces, tail, tile, 1.0 /...  90.7 us
    pallas_call x1, Pallas kernels, kernel_on_device(): pl.pallas_call(flush_kernel, out_shape=(jax.ShapeDtypeStruct(spectra.shap...  2.43 us

profile of v3, /device:TPU:0, one launch (start us, length us, event | category | flops | bytes accessed | tf_op | source)
XLA Modules:
  0.0 93.8 jit_solution(926608239540743440)
XLA Ops:
  0.6 90.7 %window_transform.1 = (f32[8,2,5,2,8192]{4,3,2,1,0:T(2,128)S(1)}, f32[8,8]{1,0:T(8,128)S(1)}) custom-call(bf16[5,96,8192]{2,1,0:T(8,128)(2,1)} %bitcast.6, f32[1,8192]{1,0:T(1,128)} %bitcast.7, s32[32]{0:T(128)} %index_hbm.1), custom_call_target="tpu_custom_call" | custom-call | tf_op jit(solution)/shard_map/window_transform/pallas_call | solution.py:647
  91.4 2.4 %flush.1 = (f32[8,2,5,2,8192]{4,3,2,1,0:T(2,128)}, f32[8,8]{1,0:T(8,128)}) custom-call(f32[8,2,5,2,8192]{4,3,2,1,0:T(2,128)S(1)} %get-tuple-element.6.spectra, f32[8,8]{1,0:T(8,128)S(1)} %get-tuple-element.7.gram), custom_call_target="tpu_custom_call" | custom-call | tf_op jit(solution)/shard_map/flush/pallas_call | solution.py:696

commit v4 on v3

--- a/solution.py
+++ b/solution.py
@@ -98,6 +98,7 @@
     half = span // 2
     short = span // tail
     common = steps - 4
+    batch = 3 if steps % 3 == 1 else 1
     lifts, lift = relay.shape[0], relay.shape[3]
     f32, bf16 = jnp.float32, jnp.bfloat16
 
@@ -158,50 +159,59 @@
                 own[block * unit:(block + 1) * unit, :] = rows.astype(bf16)
     acc[...] = jnp.zeros_like(acc)
 
-    def remote(send, recv, ssem, rsem, side, *at):
-        return pltpu.make_async_remote_copy(
-            src_ref=send.at[(side, *at)], dst_ref=recv.at[(me, *at)],
-            send_sem=ssem.at[side, at[0]], recv_sem=rsem.at[me, at[0]],
-            device_id=(px, py, sides[side]), device_id_type=MESH,
-        )
-
-    def landed(send, recv, ssem, rsem, side, *at):
-        return pltpu.make_async_remote_copy(
-            src_ref=send.at[(side, *at)], dst_ref=recv.at[(side, *at)],
-            send_sem=ssem.at[side, at[0]], recv_sem=rsem.at[side, at[0]],
-            device_id=(px, py, sides[side]), device_id_type=MESH,
-        )
-
     a_refs = (a_send, a_recv, a_ssem, a_rsem)
     n1_refs = (n1_send, n1_recv, n1_ssem, n1_rsem)
     n2_refs = (n2_send, n2_recv, n2_ssem, n2_rsem)
 
-    def m1_copy(here, side, k, n=None):
-        send, recv, ssem, rsem = m1_send.at[side, k], m1_recv.at[here, k], m1_ssem, m1_rsem
-        if n is None:
-            n = k
-        else:
-            columns = pl.ds(pl.multiple_of(n * short, short), short)
-            send, recv = send.at[:, columns], recv.at[:, columns]
-            n = steps + n + jnp.where(k == common - 1, tail, 0)
+    def batch_copy(refs, here, side, first, count):
+        send, recv, ssem, rsem = refs
+        units = pl.ds(first, count)
         return pltpu.make_async_remote_copy(
-            src_ref=send, dst_ref=recv, send_sem=ssem.at[side, n], recv_sem=rsem.at[here, n],
+            src_ref=send.at[side, units], dst_ref=recv.at[here, units],
+            send_sem=ssem.at[side, first], recv_sem=rsem.at[here, first],
             device_id=(px, py, sides[side]), device_id_type=MESH,
         )
 
-    def lifted_copy(here, side, c):
-        columns = pl.ds(c * lift, lift)
+    m1_refs = (m1_send, m1_recv, m1_ssem, m1_rsem)
+
+    def start_batch(refs, side, k):
+        @pl.when(k == 0)
+        def _():
+            batch_copy(refs, me, side, 0, 1).start()
+
+        @pl.when((k > 0) & (lax.rem(k, batch) == 0))
+        def _():
+            batch_copy(refs, me, side, k + 1 - batch, batch).start()
+
+    def wait_batch(refs, side, k):
+        @pl.when(k == 0)
+        def _():
+            batch_copy(refs, side, side, 0, 1).wait_recv()
+
+        @pl.when((k > 0) & (lax.rem(k - 1, batch) == 0))
+        def _():
+            batch_copy(refs, side, side, k, batch).wait_recv()
+
+    def wait_sent(refs, side):
+        batch_copy(refs, me, side, 0, 1).wait_send()
+
+        @pl.loop(0, (steps - 1) // batch)
+        def _(n):
+            batch_copy(refs, me, side, 1 + n * batch, batch).wait_send()
+
+    def tail_copy(here, side, k, n):
+        columns = pl.ds(pl.multiple_of(n * short, short), short)
         return pltpu.make_async_remote_copy(
-            src_ref=m1_send.at[side, 0, :, columns], dst_ref=m1_recv.at[here, 0, :, columns],
-            send_sem=lift_ssem.at[c, side], recv_sem=lift_rsem.at[c, here],
+            src_ref=m1_send.at[side, k, :, columns], dst_ref=m1_recv.at[here, k, :, columns],
+            send_sem=m1_ssem.at[side, steps + n], recv_sem=m1_rsem.at[here, steps + n],
             device_id=(px, py, sides[side]), device_id_type=MESH,
         )
 
-    def up_copy(here, side, c):
+    def up_copy(here, c):
         return pltpu.make_async_remote_copy(
-            src_ref=m1_send.at[side, 0, :, pl.ds(c * lift, lift)], dst_ref=relay.at[c, here],
-            send_sem=lift_ssem.at[c, side], recv_sem=relay_rsem.at[c, here],
-            device_id=(px, py + 1, sides[side]), device_id_type=MESH,
+            src_ref=m1_send.at[0, 0, :, pl.ds(c * lift, lift)], dst_ref=relay.at[c, here],
+            send_sem=lift_ssem.at[c], recv_sem=relay_rsem.at[c, here],
+            device_id=(px, py + 1, sides[0]), device_id_type=MESH,
         )
 
     def down_copy(side, c):
@@ -211,14 +221,11 @@
             device_id=(px, py - 1, ta), device_id_type=MESH,
         )
 
-    def goes_up(c):
-        return c < npy - 1 - py
-
     def comes_up(c):
         return (py > 0) & (c < npy - py)
 
-    def rest_copy(here, side):
-        columns = pl.ds(lifts * lift, span - lifts * lift)
+    def rest_copy(here, side, n):
+        columns = pl.ds(n * lift, span - n * lift)
         return pltpu.make_async_remote_copy(
             src_ref=m1_send.at[side, 0, :, columns], dst_ref=m1_recv.at[here, 0, :, columns],
             send_sem=m1_ssem.at[side, 0], recv_sem=m1_rsem.at[here, 0],
@@ -355,19 +362,21 @@
                         twiddle[0:2 * unit, :], k, side * half + at).astype(bf16)
                 if side == 0:
                     meet(k)
-                remote(*a_refs, side, k).start()
+
+                start_batch(a_refs, side, k)
+
+        @pl.loop(0, steps)
+        def _(k):
+            for side in range(2):
+                wait_batch(n2_refs, side, k)
 
         @pl.loop(0, steps)
         def _(j):
             k = jnp.where(
-                j < 2, common + 2 * j + 1 - me,
-                jnp.where(j < common + 2, j - 2, common + 2 * (j - common - 2) + me))
+                j < 2, common + 2 * (1 - me) + j,
+                jnp.where(j < common + 2, j - 2, 2 * me + j - 2))
             for dependent in range(2):
                 first = half * (me if dependent else 1 - me)
-                if dependent:
-                    for side in range(2):
-                        landed(*n2_refs, side, k).wait_recv()
-
                 @tiles(half)
                 def _(at):
                     product = transform(twiddle[2 * unit:6 * unit, :], k, first + at)
@@ -380,33 +389,41 @@
                                 rows = rows + n2_recv[block, k, :, pl.ds(at, tile)].astype(f32)
                             m1_send[side, k, block * unit:(block + 1) * unit, there] = rows.astype(bf16)
 
-            split = (k == common - 1) | (j == steps - 1)
-
-            @pl.when(split)
+            @pl.when(j == 1)
+            def _():
+                for side in range(2):
+                    batch_copy(m1_refs, me, side, k - 1, 2).start()
+
+            @pl.when(k == 0)
+            def _():
+                for n in range(lifts + 1):
+                    @pl.when(n == npy - 1 - py)
+                    def _():
+                        for c in range(n):
+                            up_copy(me, c).start()
+                        rest_copy(me, 0, n).start()
+                rest_copy(me, 1, 0).start()
+
+            @pl.when(k == common - 3)
+            def _():
+                for side in range(2):
+                    batch_copy(m1_refs, me, side, 1, common - 3).start()
+
+            @pl.when(k == common - 1)
+            def _():
+                for side in range(2):
+                    batch_copy(m1_refs, me, side, common - 2, 2).start()
+
+            @pl.when(j == steps - 2)
+            def _():
+                for side in range(2):
+                    batch_copy(m1_refs, me, side, k, 1).start()
+
+            @pl.when(j == steps - 1)
             def _():
                 for n in range(tail):
                     for side in range(2):
-                        m1_copy(me, side, k, n).start()
-
-            @pl.when(k == 0)
-            def _():
-                for c in range(lifts):
-                    for side in range(2):
-                        @pl.when(goes_up(c))
-                        def _():
-                            up_copy(me, side, c).start()
-
-                        @pl.when(jnp.logical_not(goes_up(c)))
-                        def _():
-                            lifted_copy(me, side, c).start()
-                for side in range(2):
-                    rest_copy(me, side).start()
-
-            @pl.when(jnp.logical_not(split) & (k != 0))
-            def _():
-                for side in range(2):
-                    m1_copy(me, side, k).start()
-
+                        tail_copy(me, side, k, n).start()
 
         weights()
         learn_of_peers()
@@ -414,8 +431,8 @@
         @pl.loop(0, steps)
         def _(k):
             for side in range(2):
-                landed(*a_refs, side, k).wait_recv()
-                landed(*n1_refs, side, k).wait_recv()
+                wait_batch(a_refs, side, k)
+                wait_batch(n1_refs, side, k)
 
             for side in range(2):
                 @tiles(half)
@@ -437,7 +454,7 @@
                 @tiles(span, 2)
                 def _(at):
                     there = pl.ds(at, tile)
-                    k = common + 2 * u + me
+                    k = common + 2 * me + u
                     both = p_recv[side, u, :, there].astype(f32) + m1_send[side, k, :, there].astype(f32)
                     add_terms(1 + side, weighted(k, at, both))
 
@@ -448,26 +465,23 @@
         gather()
         for side in range(2):
             e_copy(me, side).wait_send()
-
-        @pl.loop(0, steps)
-        def _(k):
-            for side in range(2):
-                remote(*a_refs, side, k).wait_send()
-
-                @pl.when((k != common + 2 + me) & (k != common - 1) & (k > 0))
-                def _():
-                    m1_copy(me, side, k).wait_send()
-
-        for side in range(2):
-            rest_copy(me, side).wait_send()
-            for c in range(lifts):
-                lifted_copy(me, side, c).wait_send()
-
-        @pl.loop(0, tail)
-        def _(n):
-            for side in range(2):
-                m1_copy(me, side, common - 1, n).wait_send()
-                m1_copy(me, side, common + 2 + me, n).wait_send()
+            wait_sent(a_refs, side)
+            batch_copy(m1_refs, me, side, common + 2 * (1 - me), 2).wait_send()
+            batch_copy(m1_refs, me, side, 1, common - 3).wait_send()
+            batch_copy(m1_refs, me, side, common - 2, 2).wait_send()
+            batch_copy(m1_refs, me, side, common + 2 * me, 1).wait_send()
+
+            @pl.loop(0, tail)
+            def _(n):
+                tail_copy(me, side, common + 2 * me + 1, n).wait_send()
+
+        for n in range(lifts + 1):
+            @pl.when(n == npy - 1 - py)
+            def _():
+                for c in range(n):
+                    up_copy(me, c).wait_send()
+                rest_copy(me, 0, n).wait_send()
+        rest_copy(me, 1, 0).wait_send()
 
     @pl.when(outer)
     def _():
@@ -485,7 +499,7 @@
                         twiddle[far, :], k, side * half + at).astype(bf16)
                 if side == 0:
                     meet(k)
-                remote(*n2_refs, side, k).start()
+                start_batch(n2_refs, side, k)
 
         @pl.loop(0, steps)
         def _(k):
@@ -495,9 +509,9 @@
                 for side in range(2):
                     n1_send[side, k, :, pl.ds(at, tile)] = product[side * unit:(side + 1) * unit].astype(bf16)
             for side in range(2):
-                remote(*n1_refs, side, k).start()
-            for side in range(2):
-                landed(*a_refs, side, k).wait_recv()
+                start_batch(n1_refs, side, k)
+            for side in range(2):
+                wait_batch(a_refs, side, k)
 
             @tiles(half)
             def _(at):
@@ -511,21 +525,22 @@
                         total = came + jnp.where(me == block, rows, 0.0)
                         a_send[side, k, there, here] = total.astype(bf16)
             for side in range(2):
-                remote(*a_refs, side, k).start()
+                start_batch(a_refs, side, k)
 
         weights()
 
         for c in range(lifts):
-            @pl.when(comes_up(c))
+            @pl.when(comes_up(c) & (me == 0))
             def _():
                 for side in range(2):
-                    up_copy(side, side, c).wait_recv()
+                    up_copy(side, c).wait_recv()
                     down_copy(side, c).start()
 
         for u in range(2):
             for side in range(2):
-                k = common + 2 * u + side
-                m1_copy(1 - side, 1 - side, k).wait_recv()
+                k = common + 2 * side + u
+                if u == 0:
+                    batch_copy(m1_refs, 1 - side, 1 - side, k, 2).wait_recv()
 
                 @tiles(span, 2)
                 def _(at):
@@ -552,25 +567,30 @@
                 add_terms(0, parts)
                 store(k, at, parts)
 
-        @pl.loop(0, common - 1)
+        @pl.loop(0, common)
         def _(k):
-            for side in range(2):
-                @pl.when(k == 0)
+            @pl.when(k == 0)
+            def _():
+                for n in range(lifts + 1):
+                    @pl.when((me == 0) & (n == npy - 1 - py))
+                    def _():
+                        for side in range(2):
+                            for c in range(n):
+                                down_copy(side, c).wait_recv()
+                            rest_copy(side, side, n).wait_recv()
+
+                @pl.when(me == 1)
                 def _():
-                    for c in range(lifts):
-                        lifted_copy(side, side, c).wait_recv()
-                    rest_copy(side, side).wait_recv()
-
-                @pl.when(k > 0)
+                    for side in range(2):
+                        rest_copy(side, side, 0).wait_recv()
+
+            for first, count in ((1, common - 3), (common - 2, 2)):
+                @pl.when(k == first)
                 def _():
-                    m1_copy(side, side, k).wait_recv()
+                    for side in range(2):
+                        batch_copy(m1_refs, side, side, first, count).wait_recv()
+
             arrive(k, 0, span)
-
-        @pl.loop(0, tail)
-        def _(n):
-            for side in range(2):
-                m1_copy(side, side, common - 1, n).wait_recv()
-            arrive(common - 1, n * short, short)
 
         sums = sums_of(0)
         for side in range(2):
@@ -578,30 +598,28 @@
             sums = sums + e_recv[side]
         exchange(sums)
 
-        @pl.loop(0, steps)
-        def _(k):
-            for side in range(2):
-                for refs in (a_refs, n1_refs, n2_refs):
-                    remote(*refs, side, k).wait_send()
+        for side in range(2):
+            for refs in (a_refs, n1_refs, n2_refs):
+                wait_sent(refs, side)
 
         for side in range(2):
             for u in range(2):
                 p_copy(me, side, u).wait_send()
 
         for c in range(lifts):
-            @pl.when(comes_up(c))
+            @pl.when(comes_up(c) & (me == 0))
             def _():
                 for side in range(2):
                     down_copy(side, c).wait_send()
 
         def complete(side, u, at):
-            k = common + 2 * u + side
+            k = common + 2 * side + u
             there = pl.ds(at, tile)
             store(k, at, weighted(
                 k, at, pre[side, u, :, there] + m1_recv[side, k, :, there].astype(f32)))
 
         for side in range(2):
-            m1_copy(side, side, common + side).wait_recv()
+            batch_copy(m1_refs, side, side, common + 2 * side, 1).wait_recv()
             tiles(span, 2)(functools.partial(complete, side, 0))
 
         @pl.loop(0, tail)
@@ -611,7 +629,7 @@
                 gather()
 
             for side in range(2):
-                m1_copy(side, side, common + 2 + side, n).wait_recv()
+                tail_copy(side, side, common + 2 * side + 1, n).wait_recv()
                 for c in range(0, short, tile):
                     complete(side, 1, pl.multiple_of(n * short + c, tile))
 
@@ -680,8 +698,8 @@
             dma((steps,)), dma, dma,
             dma((2, steps)), dma((2, steps)), dma((2, steps)), dma((2, steps)),
             dma((2, steps)), dma((2, steps)),
-            dma((2, steps + 2 * tail)), dma((2, steps + 2 * tail)),
-            dma((lifts, 2)), dma((lifts, 2)), dma((lifts, 2)), dma((lifts, 2)),
+            dma((2, steps + tail)), dma((2, steps + tail)),
+            dma((lifts, 2)), dma((lifts, 2)), dma((lifts,)), dma((lifts, 2)),
             dma((2, 2)), dma((2, 2)), dma((2,)), dma((2,)),
             dma((peers,)), dma((peers,)),
             pltpu.SemaphoreType.REGULAR((3,)),

time: 93.9 us -> 93.8 us (level)
  no operation moved by 1% of the time
where the time goes in v4:
time: 93.8 us; the launch traced here: 93.6 us
  Pallas kernels  93 us (99%)
    pallas_call x1, Pallas kernels, kernel_on_device(): pl.pallas_call(functools.partial(window_kernel, pieces, tail, tile, 1.0 /...  90.5 us
    pallas_call x1, Pallas kernels, kernel_on_device(): pl.pallas_call(flush_kernel, out_shape=(jax.ShapeDtypeStruct(spectra.shap...  2.43 us

profile of v4, /device:TPU:0, one launch (start us, length us, event | category | flops | bytes accessed | tf_op | source)
XLA Modules:
  0.0 93.6 jit_solution(11163272327421185358)
XLA Ops:
  0.6 90.5 %window_transform.1 = (f32[8,2,5,2,8192]{4,3,2,1,0:T(2,128)S(1)}, f32[8,8]{1,0:T(8,128)S(1)}) custom-call(bf16[5,96,8192]{2,1,0:T(8,128)(2,1)} %bitcast.6, f32[1,8192]{1,0:T(1,128)} %bitcast.7, s32[32]{0:T(128)} %index_hbm.1), custom_call_target="tpu_custom_call" | custom-call | tf_op jit(solution)/shard_map/window_transform/pallas_call | solution.py:665
  91.2 2.4 %flush.1 = (f32[8,2,5,2,8192]{4,3,2,1,0:T(2,128)}, f32[8,8]{1,0:T(8,128)}) custom-call(f32[8,2,5,2,8192]{4,3,2,1,0:T(2,128)S(1)} %get-tuple-element.6.spectra, f32[8,8]{1,0:T(8,128)S(1)} %get-tuple-element.7.gram), custom_call_target="tpu_custom_call" | custom-call | tf_op jit(solution)/shard_map/flush/pallas_call | solution.py:714

commit v5 on v4

--- a/solution.py
+++ b/solution.py
@@ -82,10 +82,10 @@
     snap_hbm, weight_hbm, index_hbm, out_ref, gram_ref,
     snap, index_ref, weight_ref, twiddle, own, root,
     a_send, a_recv, n1_send, n1_recv, n2_send, n2_recv, m1_send, m1_recv,
-    relay, p_send, p_recv, pre, e_send, e_recv, acc, gram_send, gram_recv,
+    relay, moved, p_send, p_recv, pre, e_send, e_recv, acc, gram_send, gram_recv,
     load_sem, index_sem, weight_sem,
     a_ssem, a_rsem, n1_ssem, n1_rsem, n2_ssem, n2_rsem, m1_ssem, m1_rsem,
-    relay_ssem, relay_rsem, lift_ssem, lift_rsem,
+    moved_ssem, moved_rsem, relay_ssem, relay_rsem, lift_ssem, lift_rsem,
     p_ssem, p_rsem, e_ssem, e_rsem, gram_ssem, gram_rsem, ready_sem,
 ):
     px, py, ta = lax.axis_index("px"), lax.axis_index("py"), lax.axis_index("ta")
@@ -100,12 +100,18 @@
     common = steps - 4
     batch = 3 if steps % 3 == 1 else 1
     lifts, lift = relay.shape[0], relay.shape[3]
+    shift = moved.shape[2]
+    kept, shifted = pl.ds(0, half - shift), pl.ds(half - shift, shift)
     f32, bf16 = jnp.float32, jnp.bfloat16
 
     inner = (ta == 1) | (ta == 2)
     outer = jnp.logical_not(inner)
     me = jnp.where(inner, ta - 1, ta // 3)
     sides = (jnp.where(inner, 0, 1), jnp.where(inner, 3, 2))
+
+    @pl.when(outer & (me == 0))
+    def _():
+        a_recv[:, 0, :, shifted] = jnp.zeros((2, SEGMENT_NUMBER * unit, shift), bf16)
 
     def load(k):
         there = pl.ds(pl.multiple_of(lax.rem(k, pieces) * span, span), span)
@@ -174,10 +180,41 @@
 
     m1_refs = (m1_send, m1_recv, m1_ssem, m1_rsem)
 
+    def kept_copy(here):
+        return pltpu.make_async_remote_copy(
+            src_ref=a_send.at[0, 0, :, kept], dst_ref=a_recv.at[here, 0, :, kept],
+            send_sem=a_ssem.at[0, 0], recv_sem=a_rsem.at[here, 0],
+            device_id=(px, py, sides[0]), device_id_type=MESH,
+        )
+
+    def shifted_copy(here):
+        return pltpu.make_async_remote_copy(
+            src_ref=a_send.at[0, 0, :, shifted], dst_ref=moved.at[here],
+            send_sem=moved_ssem.at[0], recv_sem=moved_rsem.at[here],
+            device_id=(px, py, sides[1]), device_id_type=MESH,
+        )
+
+    def forward_copy(here):
+        return pltpu.make_async_remote_copy(
+            src_ref=moved.at[here], dst_ref=moved.at[0],
+            send_sem=moved_ssem.at[here], recv_sem=moved_rsem.at[0],
+            device_id=(px, py, sides[1 - here]), device_id_type=MESH,
+        )
+
     def start_batch(refs, side, k):
         @pl.when(k == 0)
         def _():
-            batch_copy(refs, me, side, 0, 1).start()
+            if refs is a_refs and side == 0:
+                @pl.when(inner)
+                def _():
+                    kept_copy(me).start()
+                    shifted_copy(me).start()
+
+                @pl.when(outer)
+                def _():
+                    batch_copy(refs, me, side, 0, 1).start()
+            else:
+                batch_copy(refs, me, side, 0, 1).start()
 
         @pl.when((k > 0) & (lax.rem(k, batch) == 0))
         def _():
@@ -186,14 +223,25 @@
     def wait_batch(refs, side, k):
         @pl.when(k == 0)
         def _():
-            batch_copy(refs, side, side, 0, 1).wait_recv()
+            if refs is a_refs:
+                relays = outer & (me == 0)
+
+                @pl.when(relays)
+                def _():
+                    kept_copy(side).wait_recv()
+
+                @pl.when(jnp.logical_not(relays))
+                def _():
+                    batch_copy(refs, side, side, 0, 1).wait_recv()
+            else:
+                batch_copy(refs, side, side, 0, 1).wait_recv()
 
         @pl.when((k > 0) & (lax.rem(k - 1, batch) == 0))
         def _():
             batch_copy(refs, side, side, k, batch).wait_recv()
 
-    def wait_sent(refs, side):
-        batch_copy(refs, me, side, 0, 1).wait_send()
+    def wait_sent(refs, side, first=None):
+        (first or batch_copy(refs, me, side, 0, 1)).wait_send()
 
         @pl.loop(0, (steps - 1) // batch)
         def _(n):
@@ -434,6 +482,12 @@
                 wait_batch(a_refs, side, k)
                 wait_batch(n1_refs, side, k)
 
+            @pl.when(k == 0)
+            def _():
+                forward_copy(0).wait_recv()
+                both = a_recv[0, 0, :, shifted].astype(f32) + moved[0].astype(f32)
+                a_recv[0, 0, :, shifted] = both.astype(bf16)
+
             for side in range(2):
                 @tiles(half)
                 def _(at):
@@ -463,9 +517,10 @@
             e_copy(me, side).start()
 
         gather()
+        shifted_copy(me).wait_send()
         for side in range(2):
             e_copy(me, side).wait_send()
-            wait_sent(a_refs, side)
+            wait_sent(a_refs, side, kept_copy(me) if side == 0 else None)
             batch_copy(m1_refs, me, side, common + 2 * (1 - me), 2).wait_send()
             batch_copy(m1_refs, me, side, 1, common - 3).wait_send()
             batch_copy(m1_refs, me, side, common - 2, 2).wait_send()
@@ -512,6 +567,12 @@
                 start_batch(n1_refs, side, k)
             for side in range(2):
                 wait_batch(a_refs, side, k)
+
+            @pl.when((k == 0) & (me == 1))
+            def _():
+                for side in range(2):
+                    shifted_copy(side).wait_recv()
+                    forward_copy(side).start()
 
             @tiles(half)
             def _(at):
@@ -601,6 +662,10 @@
         for side in range(2):
             for refs in (a_refs, n1_refs, n2_refs):
                 wait_sent(refs, side)
+
+            @pl.when(me == 1)
+            def _():
+                forward_copy(side).wait_send()
 
         for side in range(2):
             for u in range(2):
@@ -657,6 +722,7 @@
     steps = variables * pieces
     lift = min(256, span // npy)
     lifts = npy - 1
+    shift = min(384, half // 2)
     bf16, f32 = jnp.bfloat16, jnp.float32
     peers = npx * npy - 1
     dma = pltpu.SemaphoreType.DMA
@@ -687,6 +753,7 @@
             pltpu.VMEM((2, steps, SEGMENT_NUMBER * unit, span), bf16),
             pltpu.VMEM((2, steps, SEGMENT_NUMBER * unit, span), bf16),
             pltpu.VMEM((lifts, 2, SEGMENT_NUMBER * unit, lift), bf16),
+            pltpu.VMEM((2, SEGMENT_NUMBER * unit, shift), bf16),
             pltpu.VMEM((2, 2, SEGMENT_NUMBER * unit, span), bf16),
             pltpu.VMEM((2, 2, SEGMENT_NUMBER * unit, span), bf16),
             pltpu.VMEM((2, 2, SEGMENT_NUMBER * unit, span), f32),
@@ -699,7 +766,7 @@
             dma((2, steps)), dma((2, steps)), dma((2, steps)), dma((2, steps)),
             dma((2, steps)), dma((2, steps)),
             dma((2, steps + tail)), dma((2, steps + tail)),
-            dma((lifts, 2)), dma((lifts, 2)), dma((lifts,)), dma((lifts, 2)),
+            dma((2,)), dma((2,)), dma((lifts, 2)), dma((lifts, 2)), dma((lifts,)), dma((lifts, 2)),
             dma((2, 2)), dma((2, 2)), dma((2,)), dma((2,)),
             dma((peers,)), dma((peers,)),
             pltpu.SemaphoreType.REGULAR((3,)),

time: 93.8 us -> 93.3 us (level)
  no operation moved by 1% of the time
where the time goes in v5:
time: 93.3 us; the launch traced here: 93.1 us
  Pallas kernels  92.5 us (99%)
    pallas_call x1, Pallas kernels, kernel_on_device(): pl.pallas_call(functools.partial(window_kernel, pieces, tail, tile, 1.0 /...  90.1 us
    pallas_call x1, Pallas kernels, kernel_on_device(): pl.pallas_call(flush_kernel, out_shape=(jax.ShapeDtypeStruct(spectra.shap...  2.43 us

profile of v5, /device:TPU:0, one launch (start us, length us, event | category | flops | bytes accessed | tf_op | source)
XLA Modules:
  0.0 93.1 jit_solution(12892634663019541308)
XLA Ops:
  0.6 90.1 %window_transform.1 = (f32[8,2,5,2,8192]{4,3,2,1,0:T(2,128)S(1)}, f32[8,8]{1,0:T(8,128)S(1)}) custom-call(bf16[5,96,8192]{2,1,0:T(8,128)(2,1)} %bitcast.6, f32[1,8192]{1,0:T(1,128)} %bitcast.7, s32[32]{0:T(128)} %index_hbm.1), custom_call_target="tpu_custom_call" | custom-call | tf_op jit(solution)/shard_map/window_transform/pallas_call | solution.py:731
  90.7 2.4 %flush.1 = (f32[8,2,5,2,8192]{4,3,2,1,0:T(2,128)}, f32[8,8]{1,0:T(8,128)}) custom-call(f32[8,2,5,2,8192]{4,3,2,1,0:T(2,128)S(1)} %get-tuple-element.6.spectra, f32[8,8]{1,0:T(8,128)S(1)} %get-tuple-element.7.gram), custom_call_target="tpu_custom_call" | custom-call | tf_op jit(solution)/shard_map/flush/pallas_call | solution.py:781

commit v6 on v5

--- a/solution.py
+++ b/solution.py
@@ -109,7 +109,9 @@
     me = jnp.where(inner, ta - 1, ta // 3)
     sides = (jnp.where(inner, 0, 1), jnp.where(inner, 3, 2))
 
-    @pl.when(outer & (me == 0))
+    moves = px == 0
+
+    @pl.when(outer & (me == 0) & moves)
     def _():
         a_recv[:, 0, :, shifted] = jnp.zeros((2, SEGMENT_NUMBER * unit, shift), bf16)
 
@@ -205,12 +207,12 @@
         @pl.when(k == 0)
         def _():
             if refs is a_refs and side == 0:
-                @pl.when(inner)
+                @pl.when(inner & moves)
                 def _():
                     kept_copy(me).start()
                     shifted_copy(me).start()
 
-                @pl.when(outer)
+                @pl.when(jnp.logical_not(inner & moves))
                 def _():
                     batch_copy(refs, me, side, 0, 1).start()
             else:
@@ -224,7 +226,7 @@
         @pl.when(k == 0)
         def _():
             if refs is a_refs:
-                relays = outer & (me == 0)
+                relays = outer & (me == 0) & moves
 
                 @pl.when(relays)
                 def _():
@@ -240,8 +242,18 @@
         def _():
             batch_copy(refs, side, side, k, batch).wait_recv()
 
-    def wait_sent(refs, side, first=None):
-        (first or batch_copy(refs, me, side, 0, 1)).wait_send()
+    def wait_sent(refs, side):
+        if refs is a_refs and side == 0:
+            @pl.when(inner & moves)
+            def _():
+                kept_copy(me).wait_send()
+                shifted_copy(me).wait_send()
+
+            @pl.when(jnp.logical_not(inner & moves))
+            def _():
+                batch_copy(refs, me, side, 0, 1).wait_send()
+        else:
+            batch_copy(refs, me, side, 0, 1).wait_send()
 
         @pl.loop(0, (steps - 1) // batch)
         def _(n):
@@ -482,7 +494,7 @@
                 wait_batch(a_refs, side, k)
                 wait_batch(n1_refs, side, k)
 
-            @pl.when(k == 0)
+            @pl.when((k == 0) & moves)
             def _():
                 forward_copy(0).wait_recv()
                 both = a_recv[0, 0, :, shifted].astype(f32) + moved[0].astype(f32)
@@ -517,10 +529,9 @@
             e_copy(me, side).start()
 
         gather()
-        shifted_copy(me).wait_send()
         for side in range(2):
             e_copy(me, side).wait_send()
-            wait_sent(a_refs, side, kept_copy(me) if side == 0 else None)
+            wait_sent(a_refs, side)
             batch_copy(m1_refs, me, side, common + 2 * (1 - me), 2).wait_send()
             batch_copy(m1_refs, me, side, 1, common - 3).wait_send()
             batch_copy(m1_refs, me, side, common - 2, 2).wait_send()
@@ -568,7 +579,7 @@
             for side in range(2):
                 wait_batch(a_refs, side, k)
 
-            @pl.when((k == 0) & (me == 1))
+            @pl.when((k == 0) & (me == 1) & moves)
             def _():
                 for side in range(2):
                     shifted_copy(side).wait_recv()
@@ -663,7 +674,7 @@
             for refs in (a_refs, n1_refs, n2_refs):
                 wait_sent(refs, side)
 
-            @pl.when(me == 1)
+            @pl.when((me == 1) & moves)
             def _():
                 forward_copy(side).wait_send()
 
@@ -722,7 +733,7 @@
     steps = variables * pieces
     lift = min(256, span // npy)
     lifts = npy - 1
-    shift = min(384, half // 2)
+    shift = min(768, half // 2)
     bf16, f32 = jnp.bfloat16, jnp.float32
     peers = npx * npy - 1
     dma = pltpu.SemaphoreType.DMA

time: 93.3 us -> 93.3 us (level)
  no operation moved by 1% of the time
where the time goes in v6:
time: 93.3 us; the launch traced here: 93.1 us
  Pallas kernels  92.5 us (99%)
    pallas_call x1, Pallas kernels, kernel_on_device(): pl.pallas_call(functools.partial(window_kernel, pieces, tail, tile, 1.0 /...  90.1 us
    pallas_call x1, Pallas kernels, kernel_on_device(): pl.pallas_call(flush_kernel, out_shape=(jax.ShapeDtypeStruct(spectra.shap...  2.43 us

profile of v6, /device:TPU:0, one launch (start us, length us, event | category | flops | bytes accessed | tf_op | source)
XLA Modules:
  0.0 93.1 jit_solution(6320820069139585454)
XLA Ops:
  0.6 90.1 %window_transform.1 = (f32[8,2,5,2,8192]{4,3,2,1,0:T(2,128)S(1)}, f32[8,8]{1,0:T(8,128)S(1)}) custom-call(bf16[5,96,8192]{2,1,0:T(8,128)(2,1)} %bitcast.6, f32[1,8192]{1,0:T(1,128)} %bitcast.7, s32[32]{0:T(128)} %index_hbm.1), custom_call_target="tpu_custom_call" | custom-call | tf_op jit(solution)/shard_map/window_transform/pallas_call | solution.py:742
  90.7 2.4 %flush.1 = (f32[8,2,5,2,8192]{4,3,2,1,0:T(2,128)}, f32[8,8]{1,0:T(8,128)}) custom-call(f32[8,2,5,2,8192]{4,3,2,1,0:T(2,128)S(1)} %get-tuple-element.6.spectra, f32[8,8]{1,0:T(8,128)S(1)} %get-tuple-element.7.gram), custom_call_target="tpu_custom_call" | custom-call | tf_op jit(solution)/shard_map/flush/pallas_call | solution.py:792

commit v7 on v5

--- a/solution.py
+++ b/solution.py
@@ -722,7 +722,7 @@
     steps = variables * pieces
     lift = min(256, span // npy)
     lifts = npy - 1
-    shift = min(384, half // 2)
+    shift = min(512, half // 2)
     bf16, f32 = jnp.bfloat16, jnp.float32
     peers = npx * npy - 1
     dma = pltpu.SemaphoreType.DMA

time: 93.3 us -> 93.2 us (level)
  no operation moved by 1% of the time
where the time goes in v7:
time: 93.2 us; the launch traced here: 93 us
  Pallas kernels  92.4 us (99%)
    pallas_call x1, Pallas kernels, kernel_on_device(): pl.pallas_call(functools.partial(window_kernel, pieces, tail, tile, 1.0 /...  90 us
    pallas_call x1, Pallas kernels, kernel_on_device(): pl.pallas_call(flush_kernel, out_shape=(jax.ShapeDtypeStruct(spectra.shap...  2.43 us

profile of v7, /device:TPU:0, one launch (start us, length us, event | category | flops | bytes accessed | tf_op | source)
XLA Modules:
  0.0 93.0 jit_solution(13403417114446694362)
XLA Ops:
  0.6 90.0 %window_transform.1 = (f32[8,2,5,2,8192]{4,3,2,1,0:T(2,128)S(1)}, f32[8,8]{1,0:T(8,128)S(1)}) custom-call(bf16[5,96,8192]{2,1,0:T(8,128)(2,1)} %bitcast.6, f32[1,8192]{1,0:T(1,128)} %bitcast.7, s32[32]{0:T(128)} %index_hbm.1), custom_call_target="tpu_custom_call" | custom-call | tf_op jit(solution)/shard_map/window_transform/pallas_call | solution.py:731
  90.6 2.4 %flush.1 = (f32[8,2,5,2,8192]{4,3,2,1,0:T(2,128)}, f32[8,8]{1,0:T(8,128)}) custom-call(f32[8,2,5,2,8192]{4,3,2,1,0:T(2,128)S(1)} %get-tuple-element.6.spectra, f32[8,8]{1,0:T(8,128)S(1)} %get-tuple-element.7.gram), custom_call_target="tpu_custom_call" | custom-call | tf_op jit(solution)/shard_map/flush/pallas_call | solution.py:781
